TPU v7x, 128 devices: a whole 4x4x4 slice. The times are simulated.
128 devices in a mesh: section: 8 (over x, core), ep: 16 (over y, z).
Axes of the slice: x: 4, y: 4, z: 4, core: 2. Of those that a mesh axis runs over, the one named last changes fastest.
Arguments:
- output_grad: bfloat16 [8, 4096, 1024], P('section', 'ep'), may hold values from -6 to 6
- layer_input: bfloat16 [8, 4096, 1024], P('section', 'ep'), may hold values from -6 to 6
- expert_ids: int32 [8, 4096, 8], P('section', 'ep'), may hold values from 0 to 63, all different within a row; in each aligned block of 256 rows (0 to 255, 256 to 511, ..., all dimensions but the last counted through in order) at most 40 rows name the same one
- route_probs: bfloat16 [8, 4096, 8], P('section', 'ep'), may hold values from 0.049804688 to 0.44921875
- gate_weight: bfloat16 [8, 64, 1024, 384], P('section', 'ep'), may hold values from -0.1875 to 0.1875
- up_weight: bfloat16 [8, 64, 1024, 384], P('section', 'ep'), may hold values from -0.1875 to 0.1875
- down_weight: bfloat16 [8, 64, 384, 1024], P('section', 'ep'), may hold values from -0.3125 to 0.3125
- saved_inputs: bfloat16 [8, 64, 640, 1024], P('section', 'ep'), may hold values from -6 to 6
- saved_gate_grad: bfloat16 [8, 64, 640, 384], P('section', 'ep'), may hold values from -0.5 to 0.5
- saved_up_grad: bfloat16 [8, 64, 640, 384], P('section', 'ep'), may hold values from -0.5 to 0.5
- saved_counts: int32 [8, 64, 16], P('section', 'ep'), may hold values from 0 to 40, as said below
Outputs:
- upstream_grad: bfloat16 [8, 4096, 1024], P('section', 'ep')
- prob_grad: bfloat16 [8, 4096, 8], P('section', 'ep')
- gate_weight_grad: bfloat16 [8, 64, 1024, 384], P('section', 'ep')
- up_weight_grad: bfloat16 [8, 64, 1024, 384], P('section', 'ep')
Inputs may be any that keep to these rules, and one draw needn't show every extreme that they name: `expert_ids`: each token names 8 different experts. Among the tokens of one device (aligned blocks of 256 tokens of a section) no expert is named more than 40 times, a bound that some block reaches. `saved_counts`: rows of a block at or beyond its count are padding; some block is full in every draw.
All inputs are finite; a program needn't handle non-finite values.
Results may differ from a plain program's by a relative error of at most 0.008.
Values may be sent and summed in bfloat16 or wider, within the bound.
A program may use at most 128 MiB of HBM per device.

v0:
```python
import functools

import jax
import jax.numpy as jnp
from jax import lax
from jax.experimental import pallas as pl
from jax.experimental.pallas import tpu as pltpu
from jax.sharding import PartitionSpec as P

MESH = pl.DeviceIdType.MESH
BF = jnp.bfloat16
F32 = jnp.float32

BATCHES = ((0, 4, 12, 1), (3, 5, 7, 13), (15, 8, 2, 9), (6, 11, 14, 10))
DONE_IN = {i: b for b, batch in enumerate(BATCHES) for i in batch}
N_SEMS = 160


def dot(a, b):
    return jnp.dot(a, b, preferred_element_type=F32)


def dot_nt(a, b):
    return lax.dot_general(a, b, (((1,), (1,)), ((), ())), preferred_element_type=F32)


def dot_tn(a, b):
    return lax.dot_general(a, b, (((0,), (0,)), ((), ())), preferred_element_type=F32)


def kernel(
    sections, cap, pad,
    g_in, x_in, m_in, wg_in, wu_in, wd_in, si_in, sg_in, su_in, cnt,
    up_out, pg_out, go_out, uo_out,
    gbuf, xbuf, meta, wg, wu, wd,
    si, sgu_raw, sgu, gov, uov,
    slots, upper, oh, xd, gd, pv, sp,
    pa, pb, s1, fin, q, t1, gin, upv,
    ppg, ppgr, ppgt,
    ssem, rsem, lsem,
):
    T, D = gbuf.shape[1], gbuf.shape[2]
    NE, FF = wg.shape[0], wg.shape[2]
    SL = si.shape[0]
    H = T // 2
    HD = D // 2
    half = (pl.ds(0, H), pl.ds(H, H))
    sec = lax.axis_index("section")
    ep = lax.axis_index("ep")
    y, z = lax.div(ep, 4), lax.rem(ep, 4)

    def at(yy, zz):
        return {"ep": lax.rem(yy, 4) * 4 + lax.rem(zz, 4)}

    nb = {
        ("y", "R"): at(y + 1, z), ("y", "L"): at(y + 3, z),
        ("z", "R"): at(y, z + 1), ("z", "L"): at(y, z + 3),
    }
    before = {"section": lax.rem(sec + sections - 1, sections)}
    after = {"section": lax.rem(sec + 1, sections)}

    ids = {}
    sent = []

    def copy(key, src, dst, dev):
        k = ids.setdefault(key, len(ids))
        return pltpu.make_async_remote_copy(
            src_ref=src, dst_ref=dst, send_sem=ssem.at[k], recv_sem=rsem.at[k],
            device_id=dev, device_id_type=MESH,
        )

    def start(c):
        c.start()
        sent.append(c)

    def load(k, src, dst):
        return pltpu.make_async_copy(src, dst, lsem.at[k])

    own = [load(0, g_in, gbuf.at[0]), load(1, x_in, xbuf.at[0]), load(2, m_in, meta.at[0])]
    for c in own:
        c.start()
    weights = [load(3, wg_in, wg), load(4, wu_in, wu), load(5, wd_in, wd)]

    def saved(e):
        return [
            load(6, si_in.at[e], si),
            load(7, sg_in.at[e], sgu_raw.at[0]),
            load(8, su_in.at[e], sgu_raw.at[1]),
        ]

    def wout(e):
        return [load(9, gov, go_out.at[e]), load(10, uov, uo_out.at[e])]

    barrier = pltpu.get_barrier_semaphore()
    for dev in (*nb.values(), before, after):
        pl.semaphore_signal(barrier, inc=1, device_id=dev, device_id_type=MESH)
    for c in saved(0):
        c.start()
    for c in weights:
        c.start()
    pl.semaphore_wait(barrier, 6)
    for c in own:
        c.wait()

    paths = (("g", gbuf, "z", "y"), ("x", xbuf, "y", "z"))
    landing = {"R": 3, "L": 1}
    order = {"R": (0, 1), "L": (1, 0)}
    early = {"R": 0, "L": 1}

    def p1(path, way, h):
        name, buf, a, _ = path
        return copy((name, "p1", way, h), buf.at[0, half[h]], buf.at[landing[way], half[h]], nb[a, way])

    def f1(path, way):
        name, buf, a, _ = path
        h = early[way]
        return copy((name, "f1", way), buf.at[landing[way], half[h]], buf.at[2, half[h]], nb[a, way])

    def p2(path, way, d, h):
        name, buf, _, b = path
        return copy(
            (name, "p2", way, d, h), buf.at[d, half[h]],
            buf.at[landing[way] * 4 + d, half[h]], nb[b, way],
        )

    def f2(path, way, d):
        name, buf, _, b = path
        h = early[way]
        return copy(
            (name, "f2", way, d), buf.at[landing[way] * 4 + d, half[h]],
            buf.at[8 + d, half[h]], nb[b, way],
        )

    def send_p2(d):
        for k in range(2):
            for path in paths:
                for way in "RL":
                    start(p2(path, way, d, order[way][k]))

    def pass_p2(d):
        for path in paths:
            for way in "RL":
                p2(path, way, d, early[way]).wait_recv()
                start(f2(path, way, d))

    def rest_p2(d):
        for path in paths:
            for way in "RL":
                p2(path, way, d, 1 - early[way]).wait_recv()

    def wait_f2(d):
        for path in paths:
            for way in "RL":
                f2(path, way, d).wait_recv()

    m1 = {w: copy(("m", "p1", w), meta.at[0], meta.at[landing[w]], nb["z", w]) for w in "RL"}
    m1f = copy(("m", "f1"), meta.at[3], meta.at[2], nb["z", "R"])
    m2 = {
        w: copy(("m", "p2", w), meta.at[pl.ds(0, 4)], meta.at[pl.ds(4 * landing[w], 4)], nb["y", w])
        for w in "RL"
    }
    m2f = copy(("m", "f2"), meta.at[pl.ds(12, 4)], meta.at[pl.ds(8, 4)], nb["y", "R"])

    for w in "RL":
        start(m1[w])
    for k in range(2):
        for path in paths:
            for way in "RL":
                start(p1(path, way, order[way][k]))
    send_p2(0)

    zero = load(11, upv, up_out)

    @pl.when(sec == sections - 1)
    def _():
        upv[...] = jnp.zeros(upv.shape, BF)
        zero.start()
        zero.wait()

    upper[...] = jnp.where(
        lax.broadcasted_iota(jnp.int32, (T, T), 0) < lax.broadcasted_iota(jnp.int32, (T, T), 1), 1.0, 0.0
    ).astype(BF)

    def weight_grads(e):
        for c in saved(e):
            c.wait()
        row = lax.broadcasted_iota(jnp.int32, (SL, 1), 0)
        live = jnp.zeros((SL, 1), F32)
        for s in range(SL // cap):
            inside = (row >= s * cap) & (row < s * cap + cnt[e, s])
            live = jnp.where(inside, 1.0, live)
        for k in range(2):
            sgu[:, pl.ds(k * FF, FF)] = (sgu_raw[k].astype(F32) * live).astype(BF)
        if e > 0:
            for c in wout(e - 1):
                c.wait()
        width = min(256, D)

        def chunk(c, _):
            cols = pl.ds(pl.multiple_of(c * width, width), width)
            both = dot_tn(si[:, cols], sgu[...]).astype(BF)
            gov[cols, :] = both[:, :FF]
            uov[cols, :] = both[:, FF:]
            return 0

        lax.fori_loop(0, D // width, chunk, 0)
        for c in wout(e):
            c.start()
        if e + 1 < NE:
            for c in saved(e + 1):
                c.start()

    def prepare(i, _):
        m = meta[i].astype(F32)
        names, probs = m[:8], m[8:]
        row = lax.broadcasted_iota(jnp.int32, (8, T), 0)
        memb = jnp.zeros((8, T), F32)
        prob = jnp.zeros((8, T), F32)
        for e in range(NE):
            here = names == (ep * NE + e).astype(F32)
            me = jnp.max(jnp.where(here, 1.0, 0.0), axis=0, keepdims=True)
            pe = jnp.sum(jnp.where(here, probs, 0.0), axis=0, keepdims=True)
            memb = jnp.where(row == e, me, memb)
            prob = jnp.where(row == e + 4, pe, prob)
        rank = dot(memb.astype(BF), upper[...])
        slots[i] = jnp.where(row < 4, jnp.where(memb > 0.5, rank, -1.0), prob)
        return 0

    def batch(b):
        code = sum(i * 16**j for j, i in enumerate(BATCHES[b]))

        def dispatch(j, p):
            i = lax.rem(lax.div(jnp.int32(code), p), 16)
            it = lax.rem(i, 4) * 4 + lax.div(i, 4)
            spot = lax.broadcasted_iota(jnp.int32, (pad, T), 0).astype(F32)
            rows = pl.ds(pl.multiple_of(j * pad, pad), pad)
            for e in range(NE):
                hit = spot == slots[i, e : e + 1, :]
                oh[i, e * pad : (e + 1) * pad, :] = jnp.where(hit, 1.0, 0.0).astype(BF)
                weight = jnp.sum(
                    jnp.where(hit, slots[i, e + 4 : e + 5, :], 0.0), axis=1, keepdims=True
                )
                pv[e, rows, :] = jnp.broadcast_to(weight, (pad, 128))
            pick = oh[i]
            gx = dot(pick, gbuf[i]).astype(BF)
            for e in range(NE):
                gd[e, rows, :] = gx[e * pad : (e + 1) * pad]
            xx = dot(pick, xbuf[it]).astype(BF)
            for e in range(NE):
                xd[e, rows, :] = xx[e * pad : (e + 1) * pad]
            return p * 16

        lax.fori_loop(0, 4, dispatch, jnp.int32(1))

        def expert(e, _):
            gate = dot(xd[e], wg[e])
            up = dot(xd[e], wu[e])
            hg = dot_nt(gd[e], wd[e])
            sigma = jax.nn.sigmoid(gate)
            active = gate * sigma
            hidden = (active * up).astype(BF).astype(F32)
            slot_prob = jnp.sum(hidden * hg, axis=1, keepdims=True)
            sp[e] = jnp.broadcast_to(slot_prob, sp.shape[1:])
            scaled = hg * pv[e][:, :1]
            gg = (scaled * up * sigma * (1.0 + gate * (1.0 - sigma))).astype(BF)
            ug = (scaled * active).astype(BF)
            xd[e] = (dot_nt(gg, wg[e]) + dot_nt(ug, wu[e])).astype(BF)
            return 0

        lax.fori_loop(0, NE, expert, 0)

        def combine(j, p):
            i = lax.rem(lax.div(jnp.int32(code), p), 16)
            it = lax.rem(i, 4) * 4 + lax.div(i, 4)
            rows = pl.ds(pl.multiple_of(j * pad, pad), pad)
            part = jnp.concatenate([xd[e, rows, :] for e in range(NE)], axis=0)
            summed = dot_tn(oh[i], part).astype(BF)
            pa[i] = summed[:, :HD]
            pb[it] = summed[:, HD:]
            spot = lax.broadcasted_iota(jnp.int32, (pad, T), 0).astype(F32)
            names = meta[i].astype(F32)[:8]
            out = jnp.zeros((8, T), F32)
            for e in range(NE):
                hit = spot == slots[i, e : e + 1, :]
                val = jnp.sum(jnp.where(hit, sp[e, rows, :][:, :1], 0.0), axis=0, keepdims=True)
                out = jnp.where(names == (ep * NE + e).astype(F32), val, out)
            ppg[i] = out
            return p * 16

        lax.fori_loop(0, 4, combine, jnp.int32(1))

    halves = (("a", pa, "y", "z", 0), ("b", pb, "z", "y", 1))

    def source(hv, da, db):
        return da * 4 + db if hv[0] == "a" else db * 4 + da

    def far(hv, way, db):
        name, part, a, _, n = hv
        h = early[way]
        return copy(
            (name, "far", way, db), part.at[8 + db, half[h]],
            s1.at[n, 0 if way == "R" else 1, db], nb[a, way],
        )

    def near(hv, way, db, h):
        name, part, a, _, n = hv
        k = 0 if way == "R" else 1
        return copy(
            (name, "near", way, db, h), part.at[(1 if way == "R" else 3) * 4 + db, half[h]],
            fin.at[n, k, db, half[h]], nb[a, way],
        )

    def far2(hv, way):
        name, _, _, b, n = hv
        h = early[way]
        return copy(
            (name, "far2", way), q.at[n, 2, half[h]], t1.at[n, 0 if way == "R" else 1], nb[b, way]
        )

    def near2(hv, way, h):
        name, _, _, b, n = hv
        k = 0 if way == "R" else 1
        return copy(
            (name, "near2", way, h), q.at[n, 1 if way == "R" else 3, half[h]],
            gin.at[n, k, half[h]], nb[b, way],
        )

    issued = set()

    def issue_ready(b, dbs):
        for db in dbs:
            for hv in halves:
                if ("f", hv[0], db) not in issued and DONE_IN[source(hv, 2, db)] <= b:
                    issued.add(("f", hv[0], db))
                    for way in "RL":
                        start(far(hv, way, db))
        for db in dbs:
            for hv in halves:
                for way in "RL":
                    da = 1 if way == "R" else 3
                    if ("n", hv[0], way, db) not in issued and DONE_IN[source(hv, da, db)] <= b:
                        issued.add(("n", hv[0], way, db))
                        start(near(hv, way, db, 1 - early[way]))

    def merge(hv, db):
        _, part, _, _, n = hv
        for way in "RL":
            h = early[way]
            k, da = (0, 1) if way == "R" else (1, 3)
            far(hv, way, db).wait_recv()
            part[da * 4 + db, half[h], :] = (
                part[da * 4 + db, half[h], :].astype(F32) + s1[n, k, db].astype(F32)
            ).astype(BF)
            start(near(hv, way, db, h))

    def total(hv, db):
        _, part, _, _, n = hv
        for way in "RL":
            for h in range(2):
                near(hv, way, db, h).wait_recv()
        return part[db].astype(F32) + fin[n, 0, db].astype(F32) + fin[n, 1, db].astype(F32)

    weight_grads(0)
    for w in "RL":
        m1[w].wait_recv()
    start(m1f)
    for path in paths:
        for way in "RL":
            p1(path, way, early[way]).wait_recv()
            start(f1(path, way))
    for path in paths:
        for way in "RL":
            p1(path, way, 1 - early[way]).wait_recv()
    m1f.wait_recv()
    for w in "RL":
        start(m2[w])
    send_p2(1)
    send_p2(3)
    weight_grads(1)
    m2["R"].wait_recv()
    start(m2f)
    weight_grads(2)
    pass_p2(0)
    for path in paths:
        for way in "RL":
            f1(path, way).wait_recv()
    send_p2(2)
    weight_grads(3)
    m2["L"].wait_recv()
    m2f.wait_recv()
    lax.fori_loop(0, 16, prepare, 0)
    for c in weights:
        c.wait()
    rest_p2(0)
    batch(0)
    pass_p2(1)
    pass_p2(3)
    rest_p2(1)
    rest_p2(3)
    batch(1)
    pass_p2(2)
    issue_ready(1, (1, 2, 3, 0))
    rest_p2(2)
    wait_f2(0)
    wait_f2(1)
    batch(2)
    issue_ready(2, (1, 2, 3, 0))
    wait_f2(3)
    wait_f2(2)
    batch(3)

    c1 = copy(("c", 1), ppg.at[pl.ds(8, 4)], ppgr.at[0], nb["y", "R"])
    cl = copy(("c", 2), ppg.at[pl.ds(4, 4)], ppgr.at[1], nb["y", "R"])
    cr = copy(("c", 3), ppg.at[pl.ds(12, 4)], ppgr.at[2], nb["y", "L"])
    c2 = copy(("c", 4), ppg.at[2], ppgt.at[0], nb["z", "R"])
    cl2 = copy(("c", 5), ppg.at[1], ppgt.at[1], nb["z", "R"])
    cr2 = copy(("c", 6), ppg.at[3], ppgt.at[2], nb["z", "L"])
    start(c1)
    start(cr)
    issue_ready(3, (2, 1, 3, 0))
    c1.wait_recv()
    ppg[pl.ds(4, 4)] = ppg[pl.ds(4, 4)] + ppgr[0]
    start(cl)
    for db in (1, 2, 3, 0):
        for hv in halves:
            merge(hv, db)
    cl.wait_recv()
    cr.wait_recv()
    ppg[pl.ds(0, 4)] = ppg[pl.ds(0, 4)] + ppgr[1] + ppgr[2]
    start(c2)
    start(cr2)
    for db in (2, 1, 3):
        for hv in halves:
            q[hv[4], db] = total(hv, db).astype(BF)
            for way in "RL":
                if db == 2:
                    start(far2(hv, way))
                elif db == (1 if way == "R" else 3):
                    start(near2(hv, way, 1 - early[way]))
    c2.wait_recv()
    ppg[1] = ppg[1] + ppgt[0]
    start(cl2)
    for hv in halves:
        n = hv[4]
        for way in "RL":
            h = early[way]
            k, db = (0, 1) if way == "R" else (1, 3)
            far2(hv, way).wait_recv()
            q[n, db, half[h], :] = (q[n, db, half[h], :].astype(F32) + t1[n, k].astype(F32)).astype(BF)
            start(near2(hv, way, h))
    cl2.wait_recv()
    cr2.wait_recv()
    pg_out[...] = ppg[0] + ppgt[1] + ppgt[2]
    ups = [
        copy(("up", n), upv.at[:, pl.ds(n * HD, HD)], up_out.at[:, pl.ds(n * HD, HD)], before)
        for n in range(2)
    ]
    for hv in halves:
        n = hv[4]
        res = total(hv, 0)
        for way in "RL":
            for h in range(2):
                near2(hv, way, h).wait_recv()
        res = res + gin[n, 0].astype(F32) + gin[n, 1].astype(F32)
        upv[:, pl.ds(n * HD, HD)] = res.astype(BF)

        @pl.when(sec > 0)
        def _():
            ups[n].start()

    for c in wout(NE - 1):
        c.wait()
    for c in sent:
        c.wait_send()
    for n in range(2):
        @pl.when(sec > 0)
        def _():
            ups[n].wait_send()

        @pl.when(sec < sections - 1)
        def _():
            ups[n].wait_recv()


def per_device(sections, og, li, ids, probs, wg, wu, wd, si, sg, su, counts):
    T, D = og.shape[1], og.shape[2]
    NE, FF = wg.shape[1], wg.shape[3]
    SL = si.shape[2]
    cap = SL // 16
    pad = -(-cap // 16) * 16
    M = 4 * pad
    HD, H = D // 2, T // 2
    meta = jnp.concatenate([ids[0].T.astype(BF), probs[0].T], axis=0)
    hbm = pl.BlockSpec(memory_space=pl.ANY)
    V = pltpu.VMEM
    up, pg, go, uo = pl.pallas_call(
        functools.partial(kernel, sections, cap, pad),
        out_shape=(
            jax.ShapeDtypeStruct((T, D), BF),
            jax.ShapeDtypeStruct((8, T), F32),
            jax.ShapeDtypeStruct((NE, D, FF), BF),
            jax.ShapeDtypeStruct((NE, D, FF), BF),
        ),
        in_specs=[hbm] * 9 + [pl.BlockSpec(memory_space=pltpu.SMEM)],
        out_specs=(hbm, pl.BlockSpec(memory_space=V), hbm, hbm),
        scratch_shapes=[
            V((16, T, D), BF), V((16, T, D), BF), V((16, 16, T), BF),
            V((NE, D, FF), BF), V((NE, D, FF), BF), V((NE, FF, D), BF),
            V((SL, D), BF), V((2, SL, FF), BF), V((SL, 2 * FF), BF), V((D, FF), BF), V((D, FF), BF),
            V((16, 8, T), F32), V((T, T), BF), V((16, M, T), BF),
            V((NE, M, D), BF), V((NE, M, D), BF), V((NE, M, 128), F32), V((NE, M, 128), F32),
            V((16, T, HD), BF), V((16, T, HD), BF),
            V((2, 2, 4, H, HD), BF), V((2, 2, 4, T, HD), BF), V((2, 4, T, HD), BF),
            V((2, 2, H, HD), BF), V((2, 2, T, HD), BF), V((T, D), BF),
            V((16, 8, T), F32), V((3, 4, 8, T), F32), V((3, 8, T), F32),
            pltpu.SemaphoreType.DMA((N_SEMS,)), pltpu.SemaphoreType.DMA((N_SEMS,)),
            pltpu.SemaphoreType.DMA((12,)),
        ],
        compiler_params=pltpu.CompilerParams(
            collective_id=0, has_side_effects=True, vmem_limit_bytes=67_000_000
        ),
    )(og[0], li[0], meta, wg[0], wu[0], wd[0], si[0], sg[0], su[0], counts[0])
    return up[None], pg.T.astype(BF)[None], go[None], uo[None]


def solution(mesh):
    return jax.shard_map(
        functools.partial(per_device, mesh.shape["section"]),
        mesh=mesh,
        in_specs=(
            P("section", "ep", None),
            P("section", "ep", None),
            P("section", "ep", None),
            P("section", "ep", None),
            P("section", "ep", None, None),
            P("section", "ep", None, None),
            P("section", "ep", None, None),
            P("section", "ep", None, None),
            P("section", "ep", None, None),
            P("section", "ep", None, None),
            P("section", "ep", None),
        ),
        out_specs=(
            P("section", "ep", None),
            P("section", "ep", None),
            P("section", "ep", None, None),
            P("section", "ep", None, None),
        ),
        check_vma=False,
    )
```

profile of v0, /device:TPU:1, one launch (start us, length us, event | category | flops | bytes accessed | tf_op | source)
XLA Modules:
  0.0 160.0 jit_solution(9873307180559912621)
XLA Ops:
  0.6 0.7 convert_bitcast_fusion.1
  1.3 1.3 pad_maximum_fusion.m_in
  2.6 148.5 %shard_map.138 = (bf16[256,1024]{1,0:T(8,128)(2,1)}, f32[8,256]{1,0:T(8,128)}, bf16[4,1024,384]{2,1,0:T(8,128)(2,1)}, bf16[4,1024,384]{2,1,0:T(8,128)(2,1)}) custom-call(bf16[256,1024]{1,0:T(8,128)(2,1)} %bitcast.31, bf16[256,1024]{1,0:T(8,128)(2,1)} %bitcast.32, bf16[16,256]{1,0:T(8,128)(2,1)} %pad_maximum_fusion.m_in, bf16[4,1024,384]{2,1,0:T(8,128)(2,1)} %bitcast.24, ...), custom_call_target="tpu_custom_call" | custom-call | tf_op jit(solution)/shard_map/pallas_call | solution.py:496
  151.1 1.3 convert_bitcast_fusion
  152.4 1.9 %copy.18 = bf16[1,256,1024]{2,1,0:T(8,128)(2,1)} copy(bf16[1,256,1024]{2,1,0:T(8,128)(2,1)} %bitcast.33) | data formatting | bytes 1048576
  154.3 0.0 copy-start
  154.3 4.0 %copy.19 = bf16[1,4,1024,384]{3,2,1,0:T(8,128)(2,1)} copy(bf16[1,4,1024,384]{3,2,1,0:T(8,128)(2,1)} %bitcast.28) | data formatting | bytes 6291456
  158.3 0.0 copy-done
  158.3 1.7 %copy.20 = bf16[1,4,1024,384]{3,2,1,0:T(8,128)(2,1)} copy(bf16[1,4,1024,384]{3,2,1,0:T(8,128)(2,1)S(1)} %bitcast.27) | data formatting | bytes 6291456
Async XLA Ops:
  154.3 4.0 %copy-start = (bf16[4,1024,384]{2,1,0:T(8,128)(2,1)S(1)}, bf16[4,1024,384]{2,1,0:T(8,128)(2,1)}, u32[]{:S(2)}) copy-start(bf16[4,1024,384]{2,1,0:T(8,128)(2,1)} %get-tuple-element.11) | copy-start | bytes 9437188
where the time goes:
time: 160 us
  Pallas kernels  148 us (92%)
  local copies, waits for them, and re-layouts  7.55 us (5%)
  other arithmetic  3.28 us (2%)
    pallas_call x1, Pallas kernels, per_device(): pl.pallas_call(functools.partial(kernel, sections, cap, pad), out_shape=(...  148 us
    unnamed x5, local copies, waits for them, and re-layouts  7.55 us

commit v1 on v0

v1 whole, which is shorter than its diff:
```python
import functools

import jax
import jax.numpy as jnp
from jax import lax
from jax.experimental import pallas as pl
from jax.experimental.pallas import tpu as pltpu
from jax.sharding import PartitionSpec as P

MESH = pl.DeviceIdType.MESH
BF = jnp.bfloat16
F32 = jnp.float32

BATCHES = ((0, 4, 12, 1), (3, 5, 7, 13), (15, 8, 2, 9), (6, 11, 14, 10))
DONE_IN = {i: b for b, batch in enumerate(BATCHES) for i in batch}
N_SEMS = 160
WAYS = ("R", "L")


def dot(a, b):
    return jnp.dot(a, b, preferred_element_type=F32)


def dot_nt(a, b):
    return lax.dot_general(a, b, (((1,), (1,)), ((), ())), preferred_element_type=F32)


def dot_tn(a, b):
    return lax.dot_general(a, b, (((0,), (0,)), ((), ())), preferred_element_type=F32)


def kernel(
    sections, cap, pad,
    g_in, x_in, m_in, wg_in, wu_in, wd_in, si_in, sg_in, su_in, cnt,
    up_out, pg_out, go_out, uo_out,
    raw, cmp, sendc, relayc, meta, wg, wu, wd,
    si, sgu_raw, sgu, gov, uov,
    memb, slots, upper, oh, xg, pv, sp, srows,
    fr, nc, pm, nm, q, t1, gin, facc, upv, ppg, ppgr,
    ssem, rsem, lsem,
):
    T, HD = raw.shape[2], raw.shape[3]
    D = 2 * HD
    NE, FF = wg.shape[0], wg.shape[2]
    SL = si.shape[0]
    H = T // 2
    QD = HD // 2
    M = NE * cap
    half = (pl.ds(0, H), pl.ds(H, H))
    sec = lax.axis_index("section")
    ep = lax.axis_index("ep")
    y, z = lax.div(ep, 4), lax.rem(ep, 4)

    def at(yy, zz):
        return {"ep": lax.rem(yy, 4) * 4 + lax.rem(zz, 4)}

    nb = {
        ("y", 0): at(y + 1, z), ("y", 1): at(y + 3, z),
        ("z", 0): at(y, z + 1), ("z", 1): at(y, z + 3),
    }
    peers = {i: at(y + i // 4, z + i % 4) for i in range(1, 16)}
    mirror = {i: (4 - i // 4) % 4 * 4 + (4 - i % 4) % 4 for i in range(1, 16)}
    before = {"section": lax.rem(sec + sections - 1, sections)}
    after = {"section": lax.rem(sec + 1, sections)}

    ids = {}
    sent = []

    def copy(key, src, dst, dev):
        k = ids.setdefault(key, len(ids))
        return pltpu.make_async_remote_copy(
            src_ref=src, dst_ref=dst, send_sem=ssem.at[k], recv_sem=rsem.at[k],
            device_id=dev, device_id_type=MESH,
        )

    def start(c):
        c.start()
        sent.append(c)

    def load(k, src, dst):
        return pltpu.make_async_copy(src, dst, lsem.at[k])

    own = [load(0, m_in, meta.at[0])] + [
        load(1 + 2 * p + ch, ref.at[:, pl.ds(ch * HD, HD)], raw.at[p, ch])
        for p, ref in enumerate((g_in, x_in)) for ch in range(2)
    ]
    for c in own:
        c.start()
    weights = [load(5, wg_in, wg), load(6, wu_in, wu), load(7, wd_in, wd)]

    def saved(e):
        return [
            load(8, si_in.at[e], si),
            load(9, sg_in.at[e], sgu_raw.at[0]),
            load(10, su_in.at[e], sgu_raw.at[1]),
        ]

    def wout(e):
        return [load(11, gov, go_out.at[e]), load(12, uov, uo_out.at[e])]

    barrier = pltpu.get_barrier_semaphore()
    for dev in (*peers.values(), before, after):
        pl.semaphore_signal(barrier, inc=1, device_id=dev, device_id_type=MESH)
    for c in saved(0):
        c.start()
    for c in weights:
        c.start()
    pl.semaphore_wait(barrier, 17)
    for c in own:
        c.wait()

    axes = (("z", "y"), ("y", "z"))
    land = (3, 1)
    both = [(p, w) for p in range(2) for w in range(2)]

    def p1(p, w, ch):
        return copy((p, "p1", w, ch), raw.at[p, ch], raw.at[p, 2 * land[w] + ch], nb[axes[p][0], w])

    def f1(p, w):
        return copy(
            (p, "f1", w), raw.at[p, 2 * land[w] + w], raw.at[p, 4 + w], nb[axes[p][0], w]
        )

    def p2(p, w, d):
        return copy(
            (p, "p2", w, d), raw.at[p, 2 * d + 1 - w], raw.at[p, 8 + 4 * w + d], nb[axes[p][1], w]
        )

    def c2(p, w, d):
        return copy((p, "c2", w, d), sendc.at[p, w, d], cmp.at[p, 4 * w + d], nb[axes[p][1], w])

    def r2(p, w, d):
        return copy((p, "r2", w, d), relayc.at[p, w, d], cmp.at[p, 8 + 4 * w + d], nb[axes[p][1], w])

    def pair(axis, w, kind, d):
        return 16 + axis * 16 + w * 8 + kind * 4 + d

    def send_p2(d):
        for p, w in both:
            start(p2(p, w, d))

    def send_c2(d):
        def pick(n, _):
            p, w = lax.div(n, 2), lax.rem(n, 2)
            sendc[p, w, d] = dot(oh[pair(p, w, 0, d)], raw[p, 2 * d + w]).astype(BF)
            return 0

        lax.fori_loop(0, 4, pick, 0)
        for p, w in both:
            start(c2(p, w, d))

    def relay(d):
        for p, w in both:
            p2(p, w, d).wait_recv()

        def pick(n, _):
            p, w = lax.div(n, 2), lax.rem(n, 2)
            relayc[p, w, d] = dot(oh[pair(p, w, 1, d)], raw[p, 8 + 4 * w + d]).astype(BF)
            return 0

        lax.fori_loop(0, 4, pick, 0)
        for p, w in both:
            start(r2(p, w, d))

    def wait_c2(d):
        for p, w in both:
            c2(p, w, d).wait_recv()

    def wait_r2(d):
        for p, w in both:
            r2(p, w, d).wait_recv()

    ms = [copy(("m", i), meta.at[0], meta.at[mirror[i]], peers[i]) for i in range(1, 16)]
    for c in ms:
        start(c)
    for k in range(2):
        for p, w in both:
            start(p1(p, w, w if k == 0 else 1 - w))
    send_p2(0)

    zero = load(13, upv, up_out)

    @pl.when(sec == sections - 1)
    def _():
        upv[...] = jnp.zeros(upv.shape, BF)
        zero.start()
        zero.wait()

    upper[...] = jnp.where(
        lax.broadcasted_iota(jnp.int32, (T, T), 0) < lax.broadcasted_iota(jnp.int32, (T, T), 1), 1.0, 0.0
    ).astype(BF)
    pv[...] = jnp.zeros(pv.shape, F32)

    def weight_grads(e):
        for c in saved(e):
            c.wait()
        row = lax.broadcasted_iota(jnp.int32, (SL, 1), 0)
        live = jnp.zeros((SL, 1), F32)
        for s in range(SL // cap):
            inside = (row >= s * cap) & (row < s * cap + cnt[e, s])
            live = jnp.where(inside, 1.0, live)
        for k in range(2):
            sgu[:, pl.ds(k * FF, FF)] = (sgu_raw[k].astype(F32) * live).astype(BF)
        if e > 0:
            for c in wout(e - 1):
                c.wait()
        width = min(256, D)

        def chunk(c, _):
            cols = pl.ds(pl.multiple_of(c * width, width), width)
            res = dot_tn(si[:, cols], sgu[...]).astype(BF)
            gov[cols, :] = res[:, :FF]
            uov[cols, :] = res[:, FF:]
            return 0

        lax.fori_loop(0, D // width, chunk, 0)
        for c in wout(e):
            c.start()
        if e + 1 < NE:
            for c in saved(e + 1):
                c.start()

    def member(n, i, owner):
        m = meta[i].astype(F32)
        names, probs = m[:8], m[8:]
        row = lax.broadcasted_iota(jnp.int32, (8, T), 0)
        is_in = jnp.zeros((8, T), F32)
        prob = jnp.zeros((8, T), F32)
        for e in range(NE):
            here = names == (owner * NE + e).astype(F32)
            me = jnp.max(jnp.where(here, 1.0, 0.0), axis=0, keepdims=True)
            pe = jnp.sum(jnp.where(here, probs, 0.0), axis=0, keepdims=True)
            is_in = jnp.where(row == e, me, is_in)
            prob = jnp.where(row == e + 4, pe, prob)
        memb[n] = is_in
        slots[n] = prob

    def member_self(n, _):
        member(n, n, ep)
        return 0

    def member_near(m, _):
        axis, w, kind, d = lax.div(m, 16), lax.rem(lax.div(m, 8), 2), lax.rem(lax.div(m, 4), 2), lax.rem(m, 4)
        d2 = kind * (3 - 2 * w)
        i = (1 - axis) * (d2 * 4 + d) + axis * (d * 4 + d2)
        step = 1 + 2 * w
        owner = lax.rem(y + (1 - axis) * step, 4) * 4 + lax.rem(z + axis * step, 4)
        member(16 + m, i, owner)
        return 0

    def one_hot(n, _):
        spot = lax.broadcasted_iota(jnp.int32, (cap, T), 0).astype(F32)
        rows = [jnp.where(spot == slots[n, e : e + 1, :], 1.0, 0.0) for e in range(NE)]
        oh[n] = jnp.concatenate(rows, axis=0).astype(BF)
        return 0

    def prepare():
        lax.fori_loop(0, 16, member_self, 0)
        lax.fori_loop(0, 32, member_near, 0)
        inside = memb[...].reshape(48 * 8, T)
        rank = dot(inside.astype(BF), upper[...])
        row = lax.rem(lax.broadcasted_iota(jnp.int32, (48 * 8, T), 0), 8)
        prob = slots[...].reshape(48 * 8, T)
        slots[...] = jnp.where(row < 4, jnp.where(inside > 0.5, rank, -1.0), prob).reshape(48, 8, T)
        lax.fori_loop(0, 48, one_hot, 0)

    def place(p, j, cols, v):
        for k in range(NE // 2):
            xg[p, 2 * k, pl.ds(j * pad, pad), cols] = v[2 * cap * k : 2 * cap * k + pad]
            xg[p, 2 * k + 1, pl.ds(j * pad, pad), cols] = v[2 * cap * (k + 1) - pad : 2 * cap * (k + 1)]

    def dispatch(p, i, j):
        d2, d = (i // 4, i % 4) if p == 0 else (i % 4, i // 4)
        low, high = pl.ds(0, HD), pl.ds(HD, HD)
        if d2 == 0:
            def pick(ch, _):
                cols = pl.ds(pl.multiple_of(ch * HD, HD), HD)
                place(p, j, cols, dot(oh[i], raw[p, 2 * d + ch]).astype(BF))
                return 0

            lax.fori_loop(0, 2, pick, 0)
        elif d2 == 3:
            place(p, j, high, dot(oh[i], raw[p, 8 + d]).astype(BF))
            place(p, j, low, cmp[p, d])
        elif d2 == 1:
            place(p, j, low, dot(oh[i], raw[p, 12 + d]).astype(BF))
            place(p, j, high, cmp[p, 4 + d])
        else:
            place(p, j, high, cmp[p, 8 + d])
            place(p, j, low, cmp[p, 12 + d])

    def batch(b):
        code = sum(i * 16**j for j, i in enumerate(BATCHES[b]))
        for j, i in enumerate(BATCHES[b]):
            for p in range(2):
                dispatch(p, i, j)

        def weigh(j, t):
            i = lax.rem(lax.div(jnp.int32(code), t), 16)
            spot = lax.broadcasted_iota(jnp.int32, (cap, T), 0).astype(F32)
            for e in range(NE):
                hit = spot == slots[i, e : e + 1, :]
                weight = jnp.sum(
                    jnp.where(hit, slots[i, e + 4 : e + 5, :], 0.0), axis=1, keepdims=True
                )
                rows = pl.ds(pl.multiple_of(j * pad + e % 2 * (pad - cap), 8), cap)
                pv[e, rows, :] = jnp.broadcast_to(weight, (cap, 128))
            return t * 16

        lax.fori_loop(0, 4, weigh, jnp.int32(1))

        def expert(e, _):
            gate = dot(xg[1, e], wg[e])
            up = dot(xg[1, e], wu[e])
            hg = dot_nt(xg[0, e], wd[e])
            sigma = jax.nn.sigmoid(gate)
            active = gate * sigma
            hidden = (active * up).astype(BF).astype(F32)
            slot_prob = jnp.sum(hidden * hg, axis=1, keepdims=True)
            sp[e] = jnp.broadcast_to(slot_prob, sp.shape[1:])
            scaled = hg * pv[e][:, :1]
            gg = (scaled * up * sigma * (1.0 + gate * (1.0 - sigma))).astype(BF)
            ug = (scaled * active).astype(BF)
            xg[1, e] = (dot_nt(gg, wg[e]) + dot_nt(ug, wu[e])).astype(BF)
            return 0

        lax.fori_loop(0, NE, expert, 0)

        def finish(j, t):
            i = lax.rem(lax.div(jnp.int32(code), t), 16)
            rows = pl.ds(pl.multiple_of(j * pad, pad), pad)
            cut = cap // 16 * 16
            for k in range(NE // 2):
                even, odd = xg[1, 2 * k, rows, :], xg[1, 2 * k + 1, rows, :]
                middle = jnp.concatenate(
                    [even[cut:].astype(F32)[:8], odd[:16].astype(F32)[8:]], axis=0
                ).astype(BF)
                o = 2 * cap * k
                srows[i, o : o + cut, :] = even[:cut]
                srows[i, o + cut : o + cut + 16, :] = middle
                srows[i, o + cut + 16 : o + 2 * cap, :] = odd[16:]
            spot = lax.broadcasted_iota(jnp.int32, (cap, T), 0).astype(F32)
            names = meta[i].astype(F32)[:8]
            out = jnp.zeros((8, T), F32)
            for e in range(NE):
                hit = spot == slots[i, e : e + 1, :]
                part = pl.ds(pl.multiple_of(j * pad + e % 2 * (pad - cap), 8), cap)
                val = jnp.sum(jnp.where(hit, sp[e, part, :][:, :1], 0.0), axis=0, keepdims=True)
                out = jnp.where(names == (ep * NE + e).astype(F32), val, out)
            ppg[i] = out
            return t * 16

        lax.fori_loop(0, 4, finish, jnp.int32(1))

    lead = (("y", "z"), ("z", "y"))

    def source(h, da, db):
        return da * 4 + db if h == 0 else db * 4 + da

    def far(h, w, db):
        return copy(
            ("far", h, w, db), srows.at[source(h, 2, db), :, pl.ds(h * HD + w * QD, QD)],
            fr.at[h, w, db], nb[lead[h][0], w],
        )

    def nearc(h, w, db):
        return copy(
            ("nc", h, w, db), srows.at[source(h, 1 + 2 * w, db), :, pl.ds(h * HD + (1 - w) * QD, QD)],
            nc.at[h, w, db], nb[lead[h][0], w],
        )

    def nearm(h, w, db):
        return copy(("nm", h, w, db), pm.at[h, w, db], nm.at[h, w, db], nb[lead[h][0], w])

    def far2(h, w):
        return copy(("far2", h, w), q.at[h, 2, half[w]], t1.at[h, w], nb[lead[h][1], w])

    def near2(h, w, k):
        return copy(
            ("near2", h, w, k), q.at[h, 1 + 2 * w, half[k]], gin.at[h, w, half[k]], nb[lead[h][1], w]
        )

    issued = set()

    def issue_ready(b, dbs):
        for kind in ("far", "near"):
            for db in dbs:
                for h, w in both:
                    da = 2 if kind == "far" else 1 + 2 * w
                    if (kind, h, w, db) not in issued and DONE_IN[source(h, da, db)] <= b:
                        issued.add((kind, h, w, db))
                        start((far if kind == "far" else nearc)(h, w, db))

    def merge(db):
        for h, w in both:
            far(h, w, db).wait_recv()

        def add(n, _):
            h, w = lax.div(n, 2), lax.rem(n, 2)
            da = 1 + 2 * w
            i = (1 - h) * (da * 4 + db) + h * (db * 4 + da)
            cols = pl.ds(pl.multiple_of(h * HD + w * QD, QD), QD)
            lhs = jnp.concatenate([oh[i], oh[pair(h, 1 - w, 1, db)]], axis=0)
            rhs = jnp.concatenate([srows[i, :, cols], fr[h, w, db]], axis=0)
            pm[h, w, db] = dot_tn(lhs, rhs).astype(BF)
            return 0

        lax.fori_loop(0, 4, add, 0)
        for h, w in both:
            start(nearm(h, w, db))

    def total(db):
        for h, w in both:
            nearc(h, w, db).wait_recv()
            nearm(h, w, db).wait_recv()

        def add(n, _):
            h, k = lax.div(n, 2), lax.rem(n, 2)
            i = (1 - h) * db + h * (db * 4)
            cols = pl.ds(pl.multiple_of(h * HD + k * QD, QD), QD)
            lhs = jnp.concatenate([oh[i], oh[pair(h, k, 0, db)]], axis=0)
            rhs = jnp.concatenate([srows[i, :, cols], nc[h, 1 - k, db]], axis=0)
            res = dot_tn(lhs, rhs) + nm[h, k, db].astype(F32)
            part = pl.ds(pl.multiple_of(k * QD, QD), QD)
            if db == 0:
                facc[h, :, part] = res
            else:
                q[h, db, :, part] = res.astype(BF)
            return 0

        lax.fori_loop(0, 4, add, 0)

    weight_grads(0)
    for c in ms:
        c.wait_recv()
    prepare()
    send_c2(0)
    for p, w in both:
        p1(p, w, w).wait_recv()
        start(f1(p, w))
    for p, w in both:
        p1(p, w, 1 - w).wait_recv()
    send_p2(1)
    send_p2(3)
    send_c2(1)
    send_c2(3)
    weight_grads(1)
    relay(0)
    for p, w in both:
        f1(p, w).wait_recv()
    send_p2(2)
    send_c2(2)
    weight_grads(2)
    for c in weights:
        c.wait()
    wait_c2(0)
    batch(0)
    relay(1)
    relay(3)
    weight_grads(3)
    wait_c2(1)
    wait_c2(3)
    batch(1)
    relay(2)
    issue_ready(1, (1, 2, 3, 0))
    wait_c2(2)
    wait_r2(0)
    wait_r2(1)
    batch(2)
    issue_ready(2, (1, 2, 3, 0))
    wait_r2(3)
    wait_r2(2)
    batch(3)
    issue_ready(3, (2, 1, 3, 0))
    pgs = [copy(("c", i), ppg.at[i], ppgr.at[mirror[i]], peers[i]) for i in range(1, 16)]
    for c in pgs:
        start(c)
    for db in (1, 2, 3, 0):
        merge(db)
    total(2)
    for h, w in both:
        start(far2(h, w))
    total(1)
    total(3)
    for h, w in both:
        start(near2(h, w, 1 - w))
    total(0)
    for h, w in both:
        db = 1 + 2 * w
        far2(h, w).wait_recv()
        q[h, db, half[w], :] = (q[h, db, half[w], :].astype(F32) + t1[h, w].astype(F32)).astype(BF)
        start(near2(h, w, w))
    for c in pgs:
        c.wait_recv()
    routed = ppg[0]
    for i in range(1, 16):
        routed = routed + ppgr[i]
    pg_out[...] = routed
    ups = [
        copy(("up", h), upv.at[:, pl.ds(h * HD, HD)], up_out.at[:, pl.ds(h * HD, HD)], before)
        for h in range(2)
    ]
    for h in range(2):
        for w in range(2):
            for k in range(2):
                near2(h, w, k).wait_recv()
        upv[:, pl.ds(h * HD, HD)] = (
            facc[h] + gin[h, 0].astype(F32) + gin[h, 1].astype(F32)
        ).astype(BF)

        @pl.when(sec > 0)
        def _():
            ups[h].start()

    for c in wout(NE - 1):
        c.wait()
    for c in sent:
        c.wait_send()
    for h in range(2):
        @pl.when(sec > 0)
        def _():
            ups[h].wait_send()

        @pl.when(sec < sections - 1)
        def _():
            ups[h].wait_recv()


def per_device(sections, og, li, ids, probs, wg, wu, wd, si, sg, su, counts):
    T, D = og.shape[1], og.shape[2]
    NE, FF = wg.shape[1], wg.shape[3]
    SL = si.shape[2]
    cap = SL // 16
    pad = -(-cap // 16) * 16
    M, R = NE * cap, 4 * pad
    HD, QD, H = D // 2, D // 4, T // 2
    meta = jnp.concatenate([ids[0].T.astype(BF), probs[0].T], axis=0)
    hbm = pl.BlockSpec(memory_space=pl.ANY)
    V = pltpu.VMEM
    up, pg, go, uo = pl.pallas_call(
        functools.partial(kernel, sections, cap, pad),
        out_shape=(
            jax.ShapeDtypeStruct((T, D), BF),
            jax.ShapeDtypeStruct((8, T), F32),
            jax.ShapeDtypeStruct((NE, D, FF), BF),
            jax.ShapeDtypeStruct((NE, D, FF), BF),
        ),
        in_specs=[hbm] * 9 + [pl.BlockSpec(memory_space=pltpu.SMEM)],
        out_specs=(hbm, pl.BlockSpec(memory_space=V), hbm, hbm),
        scratch_shapes=[
            V((2, 16, T, HD), BF), V((2, 16, M, HD), BF), V((2, 2, 4, M, HD), BF), V((2, 2, 4, M, HD), BF),
            V((16, 16, T), BF), V((NE, D, FF), BF), V((NE, D, FF), BF), V((NE, FF, D), BF),
            V((SL, D), BF), V((2, SL, FF), BF), V((SL, 2 * FF), BF), V((D, FF), BF), V((D, FF), BF),
            V((48, 8, T), F32), V((48, 8, T), F32), V((T, T), BF), V((48, M, T), BF),
            V((2, NE, R, D), BF), V((NE, R, 128), F32), V((NE, R, 128), F32), V((16, M, D), BF),
            V((2, 2, 4, M, QD), BF), V((2, 2, 4, M, QD), BF),
            V((2, 2, 4, T, QD), BF), V((2, 2, 4, T, QD), BF),
            V((2, 4, T, HD), BF), V((2, 2, H, HD), BF), V((2, 2, T, HD), BF), V((2, T, HD), F32),
            V((T, D), BF), V((16, 8, T), F32), V((16, 8, T), F32),
            pltpu.SemaphoreType.DMA((N_SEMS,)), pltpu.SemaphoreType.DMA((N_SEMS,)),
            pltpu.SemaphoreType.DMA((14,)),
        ],
        compiler_params=pltpu.CompilerParams(
            collective_id=0, has_side_effects=True, vmem_limit_bytes=67_000_000
        ),
    )(og[0], li[0], meta, wg[0], wu[0], wd[0], si[0], sg[0], su[0], counts[0])
    return up[None], pg.T.astype(BF)[None], go[None], uo[None]


def solution(mesh):
    return jax.shard_map(
        functools.partial(per_device, mesh.shape["section"]),
        mesh=mesh,
        in_specs=(
            P("section", "ep", None),
            P("section", "ep", None),
            P("section", "ep", None),
            P("section", "ep", None),
            P("section", "ep", None, None),
            P("section", "ep", None, None),
            P("section", "ep", None, None),
            P("section", "ep", None, None),
            P("section", "ep", None, None),
            P("section", "ep", None, None),
            P("section", "ep", None),
        ),
        out_specs=(
            P("section", "ep", None),
            P("section", "ep", None),
            P("section", "ep", None, None),
            P("section", "ep", None, None),
        ),
        check_vma=False,
    )
```

time: 160 us -> 140 us (0.88)
  Pallas kernels: 148 us -> 129 us
    pallas_call x1, Pallas kernels: 148 us -> 129 us  [per_device(): pl.pallas_call(functools.partial(kernel, sections, cap, pad), out_shape=(...]
where the time goes in v1:
time: 140 us
  Pallas kernels  129 us (92%)
  local copies, waits for them, and re-layouts  7.55 us (5%)
  other arithmetic  3.28 us (2%)
    pallas_call x1, Pallas kernels, per_device(): pl.pallas_call(functools.partial(kernel, sections, cap, pad), out_shape=(...  129 us
    unnamed x5, local copies, waits for them, and re-layouts  7.55 us

profile of v1, /device:TPU:1, one launch (start us, length us, event | category | flops | bytes accessed | tf_op | source)
XLA Modules:
  0.0 140.0 jit_solution(5714733004132884141)
XLA Ops:
  0.6 0.7 convert_bitcast_fusion.1
  1.3 1.3 pad_maximum_fusion.m_in
  2.6 128.6 %shard_map.138 = (bf16[256,1024]{1,0:T(8,128)(2,1)}, f32[8,256]{1,0:T(8,128)}, bf16[4,1024,384]{2,1,0:T(8,128)(2,1)}, bf16[4,1024,384]{2,1,0:T(8,128)(2,1)}) custom-call(bf16[256,1024]{1,0:T(8,128)(2,1)} %bitcast.31, bf16[256,1024]{1,0:T(8,128)(2,1)} %bitcast.32, bf16[16,256]{1,0:T(8,128)(2,1)} %pad_maximum_fusion.m_in, bf16[4,1024,384]{2,1,0:T(8,128)(2,1)} %bitcast.24, ...), custom_call_target="tpu_custom_call" | custom-call | tf_op jit(solution)/shard_map/pallas_call | solution.py:540
  131.2 1.3 convert_bitcast_fusion
  132.5 1.9 %copy.18 = bf16[1,256,1024]{2,1,0:T(8,128)(2,1)} copy(bf16[1,256,1024]{2,1,0:T(8,128)(2,1)} %bitcast.33) | data formatting | bytes 1048576
  134.4 0.0 copy-start
  134.4 4.0 %copy.19 = bf16[1,4,1024,384]{3,2,1,0:T(8,128)(2,1)} copy(bf16[1,4,1024,384]{3,2,1,0:T(8,128)(2,1)} %bitcast.28) | data formatting | bytes 6291456
  138.4 0.0 copy-done
  138.4 1.7 %copy.20 = bf16[1,4,1024,384]{3,2,1,0:T(8,128)(2,1)} copy(bf16[1,4,1024,384]{3,2,1,0:T(8,128)(2,1)S(1)} %bitcast.27) | data formatting | bytes 6291456
Async XLA Ops:
  134.4 4.0 %copy-start = (bf16[4,1024,384]{2,1,0:T(8,128)(2,1)S(1)}, bf16[4,1024,384]{2,1,0:T(8,128)(2,1)}, u32[]{:S(2)}) copy-start(bf16[4,1024,384]{2,1,0:T(8,128)(2,1)} %get-tuple-element.11) | copy-start | bytes 9437188

commit v2 on v1

--- a/solution.py
+++ b/solution.py
@@ -11,9 +11,9 @@
 BF = jnp.bfloat16
 F32 = jnp.float32
 
-BATCHES = ((0, 4, 12, 1), (3, 5, 7, 13), (15, 8, 2, 9), (6, 11, 14, 10))
+BATCHES = ((4, 12, 1, 3), (8, 2, 5, 0), (7, 13, 15), (9, 6), (11, 14, 10))
 DONE_IN = {i: b for b, batch in enumerate(BATCHES) for i in batch}
-N_SEMS = 160
+N_SEMS = 176
 WAYS = ("R", "L")
 
 
@@ -31,17 +31,17 @@
 
 def kernel(
     sections, cap, pad,
-    g_in, x_in, m_in, wg_in, wu_in, wd_in, si_in, sg_in, su_in, cnt,
+    g_in, x_in, ids_in, prob_in, wg_in, wu_in, wd_in, si_in, sg_in, su_in, cnt,
     up_out, pg_out, go_out, uo_out,
-    raw, cmp, sendc, relayc, meta, wg, wu, wd,
-    si, sgu_raw, sgu, gov, uov,
+    raw, cmp, sendc, relayc, meta, wgu, wd,
+    si, sgu_raw, sgu,
     memb, slots, upper, oh, xg, pv, sp, srows,
     fr, nc, pm, nm, q, t1, gin, facc, upv, ppg, ppgr,
     ssem, rsem, lsem,
 ):
     T, HD = raw.shape[2], raw.shape[3]
     D = 2 * HD
-    NE, FF = wg.shape[0], wg.shape[2]
+    NE, FF = wd.shape[0], wd.shape[1]
     SL = si.shape[0]
     H = T // 2
     QD = HD // 2
@@ -80,13 +80,17 @@
     def load(k, src, dst):
         return pltpu.make_async_copy(src, dst, lsem.at[k])
 
-    own = [load(0, m_in, meta.at[0])] + [
+    own = [
         load(1 + 2 * p + ch, ref.at[:, pl.ds(ch * HD, HD)], raw.at[p, ch])
         for p, ref in enumerate((g_in, x_in)) for ch in range(2)
     ]
     for c in own:
         c.start()
-    weights = [load(5, wg_in, wg), load(6, wu_in, wu), load(7, wd_in, wd)]
+    weights = [
+        load(5, wg_in, wgu.at[:, :, pl.ds(0, FF)]),
+        load(6, wu_in, wgu.at[:, :, pl.ds(FF, FF)]),
+        load(7, wd_in, wd),
+    ]
 
     def saved(e):
         return [
@@ -94,9 +98,6 @@
             load(9, sg_in.at[e], sgu_raw.at[0]),
             load(10, su_in.at[e], sgu_raw.at[1]),
         ]
-
-    def wout(e):
-        return [load(11, gov, go_out.at[e]), load(12, uov, uo_out.at[e])]
 
     barrier = pltpu.get_barrier_semaphore()
     for dev in (*peers.values(), before, after):
@@ -105,6 +106,7 @@
         c.start()
     for c in weights:
         c.start()
+    meta[0] = jnp.concatenate([ids_in[...].astype(F32), prob_in[...].astype(F32)], axis=0).astype(BF)
     pl.semaphore_wait(barrier, 17)
     for c in own:
         c.wait()
@@ -178,13 +180,9 @@
             start(p1(p, w, w if k == 0 else 1 - w))
     send_p2(0)
 
-    zero = load(13, upv, up_out)
-
     @pl.when(sec == sections - 1)
     def _():
-        upv[...] = jnp.zeros(upv.shape, BF)
-        zero.start()
-        zero.wait()
+        up_out[...] = jnp.zeros(up_out.shape, BF)
 
     upper[...] = jnp.where(
         lax.broadcasted_iota(jnp.int32, (T, T), 0) < lax.broadcasted_iota(jnp.int32, (T, T), 1), 1.0, 0.0
@@ -201,21 +199,16 @@
             live = jnp.where(inside, 1.0, live)
         for k in range(2):
             sgu[:, pl.ds(k * FF, FF)] = (sgu_raw[k].astype(F32) * live).astype(BF)
-        if e > 0:
-            for c in wout(e - 1):
-                c.wait()
         width = min(256, D)
 
         def chunk(c, _):
             cols = pl.ds(pl.multiple_of(c * width, width), width)
             res = dot_tn(si[:, cols], sgu[...]).astype(BF)
-            gov[cols, :] = res[:, :FF]
-            uov[cols, :] = res[:, FF:]
+            go_out[e, cols, :] = res[:, :FF]
+            uo_out[e, cols, :] = res[:, FF:]
             return 0
 
         lax.fori_loop(0, D // width, chunk, 0)
-        for c in wout(e):
-            c.start()
         if e + 1 < NE:
             for c in saved(e + 1):
                 c.start()
@@ -291,6 +284,8 @@
 
     def batch(b):
         code = sum(i * 16**j for j, i in enumerate(BATCHES[b]))
+        count = len(BATCHES[b])
+        used = pl.ds(0, count * pad)
         for j, i in enumerate(BATCHES[b]):
             for p in range(2):
                 dispatch(p, i, j)
@@ -307,21 +302,21 @@
                 pv[e, rows, :] = jnp.broadcast_to(weight, (cap, 128))
             return t * 16
 
-        lax.fori_loop(0, 4, weigh, jnp.int32(1))
+        lax.fori_loop(0, count, weigh, jnp.int32(1))
 
         def expert(e, _):
-            gate = dot(xg[1, e], wg[e])
-            up = dot(xg[1, e], wu[e])
-            hg = dot_nt(xg[0, e], wd[e])
+            gate_up = dot(xg[1, e, used, :], wgu[e])
+            gate, up = gate_up[:, :FF], gate_up[:, FF:]
+            hg = dot_nt(xg[0, e, used, :], wd[e])
             sigma = jax.nn.sigmoid(gate)
             active = gate * sigma
             hidden = (active * up).astype(BF).astype(F32)
             slot_prob = jnp.sum(hidden * hg, axis=1, keepdims=True)
-            sp[e] = jnp.broadcast_to(slot_prob, sp.shape[1:])
-            scaled = hg * pv[e][:, :1]
+            sp[e, used, :] = jnp.broadcast_to(slot_prob, (count * pad, 128))
+            scaled = hg * pv[e, used, :][:, :1]
             gg = (scaled * up * sigma * (1.0 + gate * (1.0 - sigma))).astype(BF)
             ug = (scaled * active).astype(BF)
-            xg[1, e] = (dot_nt(gg, wg[e]) + dot_nt(ug, wu[e])).astype(BF)
+            xg[1, e, used, :] = dot_nt(jnp.concatenate([gg, ug], axis=1), wgu[e]).astype(BF)
             return 0
 
         lax.fori_loop(0, NE, expert, 0)
@@ -350,7 +345,7 @@
             ppg[i] = out
             return t * 16
 
-        lax.fori_loop(0, 4, finish, jnp.int32(1))
+        lax.fori_loop(0, count, finish, jnp.int32(1))
 
     lead = (("y", "z"), ("z", "y"))
 
@@ -372,12 +367,18 @@
     def nearm(h, w, db):
         return copy(("nm", h, w, db), pm.at[h, w, db], nm.at[h, w, db], nb[lead[h][0], w])
 
-    def far2(h, w):
-        return copy(("far2", h, w), q.at[h, 2, half[w]], t1.at[h, w], nb[lead[h][1], w])
-
-    def near2(h, w, k):
+    def cols_of(c):
+        return pl.ds(c * QD, QD)
+
+    def far2(h, w, c):
         return copy(
-            ("near2", h, w, k), q.at[h, 1 + 2 * w, half[k]], gin.at[h, w, half[k]], nb[lead[h][1], w]
+            ("far2", h, w, c), q.at[h, 2, half[w], cols_of(c)], t1.at[h, w, :, cols_of(c)], nb[lead[h][1], w]
+        )
+
+    def near2(h, w, k, c):
+        return copy(
+            ("near2", h, w, k, c), q.at[h, 1 + 2 * w, half[k], cols_of(c)],
+            gin.at[h, w, half[k], cols_of(c)], nb[lead[h][1], w],
         )
 
     issued = set()
@@ -446,84 +447,103 @@
     send_c2(3)
     weight_grads(1)
     relay(0)
+    for c in weights:
+        c.wait()
+    wait_c2(0)
+    batch(0)
     for p, w in both:
         f1(p, w).wait_recv()
     send_p2(2)
     send_c2(2)
-    weight_grads(2)
-    for c in weights:
-        c.wait()
-    wait_c2(0)
-    batch(0)
     relay(1)
     relay(3)
+    weight_grads(2)
     weight_grads(3)
+    wait_r2(0)
     wait_c2(1)
+    batch(1)
     wait_c2(3)
-    batch(1)
+    batch(2)
     relay(2)
-    issue_ready(1, (1, 2, 3, 0))
+    issue_ready(2, (0, 1, 3, 2))
     wait_c2(2)
-    wait_r2(0)
     wait_r2(1)
-    batch(2)
-    issue_ready(2, (1, 2, 3, 0))
+    batch(3)
+    issue_ready(3, (1, 0, 3, 2))
     wait_r2(3)
     wait_r2(2)
-    batch(3)
-    issue_ready(3, (2, 1, 3, 0))
+    batch(4)
+    issue_ready(4, (2, 3, 1, 0))
+    merge(0)
+    merge(1)
+    merge(2)
+    merge(3)
     pgs = [copy(("c", i), ppg.at[i], ppgr.at[mirror[i]], peers[i]) for i in range(1, 16)]
     for c in pgs:
         start(c)
-    for db in (1, 2, 3, 0):
-        merge(db)
+    total(0)
+    total(1)
     total(2)
-    for h, w in both:
-        start(far2(h, w))
-    total(1)
+    for c in range(2):
+        for h, w in both:
+            start(far2(h, w, c))
     total(3)
-    for h, w in both:
-        start(near2(h, w, 1 - w))
-    total(0)
-    for h, w in both:
-        db = 1 + 2 * w
-        far2(h, w).wait_recv()
-        q[h, db, half[w], :] = (q[h, db, half[w], :].astype(F32) + t1[h, w].astype(F32)).astype(BF)
-        start(near2(h, w, w))
+    for c in range(2):
+        for h, w in both:
+            start(near2(h, w, 1 - w, c))
+        for h, w in both:
+            far2(h, w, c).wait_recv()
+            db = 1 + 2 * w
+            q[h, db, half[w], cols_of(c)] = (
+                q[h, db, half[w], cols_of(c)].astype(F32) + t1[h, w, :, cols_of(c)].astype(F32)
+            ).astype(BF)
+            start(near2(h, w, w, c))
     for c in pgs:
         c.wait_recv()
     routed = ppg[0]
     for i in range(1, 16):
         routed = routed + ppgr[i]
     pg_out[...] = routed
-    ups = [
-        copy(("up", h), upv.at[:, pl.ds(h * HD, HD)], up_out.at[:, pl.ds(h * HD, HD)], before)
-        for h in range(2)
-    ]
-    for h in range(2):
-        for w in range(2):
-            for k in range(2):
-                near2(h, w, k).wait_recv()
-        upv[:, pl.ds(h * HD, HD)] = (
-            facc[h] + gin[h, 0].astype(F32) + gin[h, 1].astype(F32)
-        ).astype(BF)
-
+    ups = {}
+    for c in range(2):
+        for h in range(2):
+            for w in range(2):
+                for k in range(2):
+                    near2(h, w, k, c).wait_recv()
+            cols = pl.ds(h * HD + c * QD, QD)
+            upv[:, cols] = (
+                facc[h, :, cols_of(c)]
+                + gin[h, 0, :, cols_of(c)].astype(F32)
+                + gin[h, 1, :, cols_of(c)].astype(F32)
+            ).astype(BF)
+            ups[h, c] = copy(("up", h, c), upv.at[:, cols], up_out.at[:, cols], before)
+
+            @pl.when(sec > 0)
+            def _():
+                ups[h, c].start()
+
+    for c in sent:
+        c.wait_send()
+    for c in ups.values():
         @pl.when(sec > 0)
         def _():
-            ups[h].start()
-
-    for c in wout(NE - 1):
-        c.wait()
-    for c in sent:
-        c.wait_send()
-    for h in range(2):
-        @pl.when(sec > 0)
-        def _():
-            ups[h].wait_send()
+            c.wait_send()
 
         @pl.when(sec < sections - 1)
         def _():
-            ups[h].wait_recv()
+            c.wait_recv()
+
+
+def deliver(up_in, pg_in, go_in, uo_in, up_out, pg_out, go_out, uo_out, sem):
+    out = [(up_in, up_out)]
+    for e in range(go_in.shape[0]):
+        out += [(go_in.at[e], go_out.at[e]), (uo_in.at[e], uo_out.at[e])]
+    out = [pltpu.make_async_copy(v, o, sem.at[k]) for k, (v, o) in enumerate(out)]
+    for c in out:
+        c.start()
+    pg_out[...] = pg_in[...].astype(BF)
+    for c in out:
+        c.wait()
 
 
 def per_device(sections, og, li, ids, probs, wg, wu, wd, si, sg, su, counts):
@@ -534,23 +554,22 @@
     pad = -(-cap // 16) * 16
     M, R = NE * cap, 4 * pad
     HD, QD, H = D // 2, D // 4, T // 2
-    meta = jnp.concatenate([ids[0].T.astype(BF), probs[0].T], axis=0)
     hbm = pl.BlockSpec(memory_space=pl.ANY)
     V = pltpu.VMEM
     up, pg, go, uo = pl.pallas_call(
         functools.partial(kernel, sections, cap, pad),
         out_shape=(
-            jax.ShapeDtypeStruct((T, D), BF),
-            jax.ShapeDtypeStruct((8, T), F32),
-            jax.ShapeDtypeStruct((NE, D, FF), BF),
-            jax.ShapeDtypeStruct((NE, D, FF), BF),
+            V((T, D), BF),
+            V((8, T), F32),
+            V((NE, D, FF), BF),
+            V((NE, D, FF), BF),
         ),
-        in_specs=[hbm] * 9 + [pl.BlockSpec(memory_space=pltpu.SMEM)],
-        out_specs=(hbm, pl.BlockSpec(memory_space=V), hbm, hbm),
+        in_specs=[hbm] * 2 + [pl.BlockSpec(memory_space=V)] * 2 + [hbm] * 6 + [pl.BlockSpec(memory_space=pltpu.SMEM)],
+        out_specs=(pl.BlockSpec(memory_space=V),) * 4,
         scratch_shapes=[
             V((2, 16, T, HD), BF), V((2, 16, M, HD), BF), V((2, 2, 4, M, HD), BF), V((2, 2, 4, M, HD), BF),
-            V((16, 16, T), BF), V((NE, D, FF), BF), V((NE, D, FF), BF), V((NE, FF, D), BF),
-            V((SL, D), BF), V((2, SL, FF), BF), V((SL, 2 * FF), BF), V((D, FF), BF), V((D, FF), BF),
+            V((16, 16, T), BF), V((NE, D, 2 * FF), BF), V((NE, FF, D), BF),
+            V((SL, D), BF), V((2, SL, FF), BF), V((SL, 2 * FF), BF),
             V((48, 8, T), F32), V((48, 8, T), F32), V((T, T), BF), V((48, M, T), BF),
             V((2, NE, R, D), BF), V((NE, R, 128), F32), V((NE, R, 128), F32), V((16, M, D), BF),
             V((2, 2, 4, M, QD), BF), V((2, 2, 4, M, QD), BF),
@@ -561,10 +580,23 @@
             pltpu.SemaphoreType.DMA((14,)),
         ],
         compiler_params=pltpu.CompilerParams(
-            collective_id=0, has_side_effects=True, vmem_limit_bytes=67_000_000
+            collective_id=0, has_side_effects=True, vmem_limit_bytes=59_800_000
         ),
-    )(og[0], li[0], meta, wg[0], wu[0], wd[0], si[0], sg[0], su[0], counts[0])
-    return up[None], pg.T.astype(BF)[None], go[None], uo[None]
+    )(og[0], li[0], ids[0].T, probs[0].T, wg[0], wu[0], wd[0], si[0], sg[0], su[0], counts[0])
+    up, pg, go, uo = pl.pallas_call(
+        deliver,
+        out_shape=(
+            jax.ShapeDtypeStruct((T, D), BF),
+            jax.ShapeDtypeStruct((8, T), BF),
+            jax.ShapeDtypeStruct((NE, D, FF), BF),
+            jax.ShapeDtypeStruct((NE, D, FF), BF),
+        ),
+        in_specs=[pl.BlockSpec(memory_space=V)] * 4,
+        out_specs=(hbm, pl.BlockSpec(memory_space=V), hbm, hbm),
+        scratch_shapes=[pltpu.SemaphoreType.DMA((1 + 2 * NE,))],
+        compiler_params=pltpu.CompilerParams(vmem_limit_bytes=16 * 2**20),
+    )(up, pg, go, uo)
+    return up[None], pg.T[None], go[None], uo[None]
 
 
 def solution(mesh):

time: 140 us -> 130 us (0.929)
  local copies, waits for them, and re-layouts: 7.55 us -> 0 us
  other arithmetic: 3.28 us -> 0 us
    unnamed x5 -> x0, local copies, waits for them, and re-layouts: 7.55 us -> none
    pallas_call x0 -> x1, Pallas kernels: none -> 3.49 us  [per_device(): pl.pallas_call(deliver, out_shape=(jax.ShapeDtypeStruct((T, D), BF), jax....]
    pallas_call x1, Pallas kernels: 129 us -> 125 us  [per_device(): pl.pallas_call(functools.partial(kernel, sections, cap, pad), out_shape=(...]
where the time goes in v2:
time: 130 us
  Pallas kernels  129 us (99%)
    pallas_call x1, Pallas kernels, per_device(): pl.pallas_call(functools.partial(kernel, sections, cap, pad), out_shape=(...  125 us
    pallas_call x1, Pallas kernels, per_device(): pl.pallas_call(deliver, out_shape=(jax.ShapeDtypeStruct((T, D), BF), jax....  3.49 us

profile of v2, /device:TPU:1, one launch (start us, length us, event | category | flops | bytes accessed | tf_op | source)
XLA Modules:
  0.0 129.5 jit_solution(6682360003933780152)
XLA Ops:
  0.6 125.4 %shard_map.138 = (bf16[256,1024]{1,0:T(8,128)(2,1)S(1)}, f32[8,256]{1,0:T(8,128)S(1)}, bf16[4,1024,384]{2,1,0:T(8,128)(2,1)S(1)}, bf16[4,1024,384]{2,1,0:T(8,128)(2,1)S(1)}) custom-call(bf16[256,1024]{1,0:T(8,128)(2,1)} %bitcast.27, bf16[256,1024]{1,0:T(8,128)(2,1)} %bitcast.28, s32[8,256]{1,0:T(8,128)} %bitcast.29, bf16[8,256]{1,0:T(8,128)(2,1)} %bitcast.30, ...), custom_call_target="tpu_custom_call" | custom-call | tf_op jit(solution)/shard_map/pallas_call | solution.py:559
  126.0 3.5 %shard_map.139 = (bf16[256,1024]{1,0:T(8,128)(2,1)}, bf16[8,256]{1,0:T(8,128)(2,1)}, bf16[4,1024,384]{2,1,0:T(8,128)(2,1)}, bf16[4,1024,384]{2,1,0:T(8,128)(2,1)}) custom-call(bf16[256,1024]{1,0:T(8,128)(2,1)S(1)} %get-tuple-element.12.up_in, f32[8,256]{1,0:T(8,128)S(1)} %get-tuple-element.13.pg_in, bf16[4,1024,384]{2,1,0:T(8,128)(2,1)S(1)} %get-tuple-element.14.go_in, ...), custom_call_target="tpu_custom_call" | custom-call | tf_op jit(solution)/shard_map/pallas_call | solution.py:586

commit v3 on v2

v3 whole, which is shorter than its diff:
```python
import functools

import jax
import jax.numpy as jnp
from jax import lax
from jax.experimental import pallas as pl
from jax.experimental.pallas import tpu as pltpu
from jax.sharding import PartitionSpec as P

MESH = pl.DeviceIdType.MESH
BF = jnp.bfloat16
F32 = jnp.float32

RAW = ((0, 0), (0, 1), (1, 0), (0, 2), (2, 0), (2, 3))
RAW_PARENT = (None, 0, 0, 1, 2, 4)
LEAF = ((0, 3), (3, 0), (1, 1), (3, 1), (1, 3), (1, 2), (3, 2), (2, 1), (2, 2), (3, 3))
LEAF_PARENT = (0, 0, 1, 1, 2, 3, 3, 4, 5, 5)
NL = len(LEAF)
IMAGES = range(4)
BATCHES = ((0, 1, 3, 4, 12), (7, 13, 2, 8), (5, 15, 10), (6, 14, 9, 11))
PAIRS = 16 + 4 * NL
N_SEMS = 224
CHUNKS = 2


def image(v, node):
    dy, dz = node if v < 2 else node[::-1]
    return ((-dy) % 4, (-dz) % 4) if v % 2 else (dy, dz)


def image_at(v, node):
    swap, flip = lax.div(v, 2), lax.rem(v, 2)
    dy = (1 - swap) * node[0] + swap * node[1]
    dz = (1 - swap) * node[1] + swap * node[0]
    return lax.rem((1 - flip) * dy + flip * (4 - dy), 4), lax.rem((1 - flip) * dz + flip * (4 - dz), 4)


def minus(node):
    return (-node[0]) % 4, (-node[1]) % 4


def step(parent, child):
    return (child[0] - parent[0]) % 4, (child[1] - parent[1]) % 4


def dot(a, b):
    return jnp.dot(a, b, preferred_element_type=F32)


def dot_nt(a, b):
    return lax.dot_general(a, b, (((1,), (1,)), ((), ())), preferred_element_type=F32)


def dot_tn(a, b):
    return lax.dot_general(a, b, (((0,), (0,)), ((), ())), preferred_element_type=F32)


def kernel(
    sections, cap, pad,
    g_in, x_in, ids_in, prob_in, wg_in, wu_in, wd_in, si_in, sg_in, su_in, cnt,
    up_out, pg_out, go_out, uo_out,
    raw, cmp, sendc, meta, wgu, wd,
    si, sgu_raw, sgu,
    memb, slots, upper, oh, xg, pv, sp, srows,
    fr, pm, nm, upv, ppg, ppgr,
    ssem, rsem, lsem,
):
    T, HD = raw.shape[2], raw.shape[3]
    D = 2 * HD
    NE, FF = wd.shape[0], wd.shape[1]
    SL = si.shape[0]
    QD = HD // 2
    M = NE * cap
    TC = T // CHUNKS
    sec = lax.axis_index("section")
    ep = lax.axis_index("ep")
    y, z = lax.div(ep, 4), lax.rem(ep, 4)

    def at(yy, zz):
        return {"ep": lax.rem(yy, 4) * 4 + lax.rem(zz, 4)}

    peers = {i: at(y + i // 4, z + i % 4) for i in range(1, 16)}
    mirror = {i: (4 - i // 4) % 4 * 4 + (4 - i % 4) % 4 for i in range(1, 16)}
    before = {"section": lax.rem(sec + sections - 1, sections)}
    after = {"section": lax.rem(sec + 1, sections)}

    ids = {}
    sent = []

    def copy(key, src, dst, dev):
        k = ids.setdefault(key, len(ids))
        return pltpu.make_async_remote_copy(
            src_ref=src, dst_ref=dst, send_sem=ssem.at[k], recv_sem=rsem.at[k],
            device_id=dev, device_id_type=MESH,
        )

    def start(c):
        c.start()
        sent.append(c)

    def load(k, src, dst):
        return pltpu.make_async_copy(src, dst, lsem.at[k])

    own = [
        load(1 + 2 * p + ch, ref.at[:, pl.ds(ch * HD, HD)], raw.at[2 * p + ch, 0])
        for p, ref in enumerate((g_in, x_in)) for ch in range(2)
    ]
    for c in own:
        c.start()
    weights = [
        load(5, wg_in, wgu.at[:, :, pl.ds(0, FF)]),
        load(6, wu_in, wgu.at[:, :, pl.ds(FF, FF)]),
        load(7, wd_in, wd),
    ]

    def saved(e):
        return [
            load(8, si_in.at[e], si),
            load(9, sg_in.at[e], sgu_raw.at[0]),
            load(10, su_in.at[e], sgu_raw.at[1]),
        ]

    barrier = pltpu.get_barrier_semaphore()
    for dev in (*peers.values(), before, after):
        pl.semaphore_signal(barrier, inc=1, device_id=dev, device_id_type=MESH)
    for c in saved(0):
        c.start()
    for c in weights:
        c.start()
    meta[0] = jnp.concatenate([ids_in[...].astype(F32), prob_in[...].astype(F32)], axis=0).astype(BF)
    pl.semaphore_wait(barrier, 17)
    for c in own:
        c.wait()

    def toward(v, parent, child):
        dy, dz = image(v, step(parent, child))
        return at(y + dy, z + dz)

    def source(v, node):
        dy, dz = image(v, minus(node))
        return dy * 4 + dz

    def source_at(v, node):
        dy, dz = image_at(v, minus(node))
        return dy * 4 + dz

    def raw_down(v, k):
        r = RAW_PARENT[k]
        return copy(("raw", v, k), raw.at[v, r], raw.at[v, k], toward(v, RAW[r], RAW[k]))

    def leaf_down(v, l):
        return copy(("leaf", v, l), sendc.at[v, l], cmp.at[v, l], toward(v, RAW[LEAF_PARENT[l]], LEAF[l]))

    def send_leaf(*ls):
        for l in ls:
            def pick(v, _):
                sendc[v, l] = dot(oh[16 + v * NL + l], raw[v, LEAF_PARENT[l]]).astype(BF)
                return 0

            lax.fori_loop(0, 4, pick, 0)
            for v in IMAGES:
                start(leaf_down(v, l))

    def wait_raw(*ks):
        for k in ks:
            for v in IMAGES:
                raw_down(v, k).wait_recv()

    def wait_leaf(*ls):
        for l in ls:
            for v in IMAGES:
                leaf_down(v, l).wait_recv()

    def pass_raw(k, child):
        for v in IMAGES:
            raw_down(v, k).wait_recv()
            start(raw_down(v, child))

    ms = [copy(("m", i), meta.at[0], meta.at[mirror[i]], peers[i]) for i in range(1, 16)]
    for c in ms:
        start(c)
    for k in (1, 2):
        for v in IMAGES:
            start(raw_down(v, k))

    @pl.when(sec == sections - 1)
    def _():
        up_out[...] = jnp.zeros(up_out.shape, BF)

    upper[...] = jnp.where(
        lax.broadcasted_iota(jnp.int32, (T, T), 0) < lax.broadcasted_iota(jnp.int32, (T, T), 1), 1.0, 0.0
    ).astype(BF)
    pv[...] = jnp.zeros(pv.shape, F32)

    def weight_grads(e):
        for c in saved(e):
            c.wait()
        row = lax.broadcasted_iota(jnp.int32, (SL, 1), 0)
        live = jnp.zeros((SL, 1), F32)
        for s in range(SL // cap):
            inside = (row >= s * cap) & (row < s * cap + cnt[e, s])
            live = jnp.where(inside, 1.0, live)
        for k in range(2):
            sgu[:, pl.ds(k * FF, FF)] = (sgu_raw[k].astype(F32) * live).astype(BF)
        width = min(256, D)

        def chunk(c, _):
            cols = pl.ds(pl.multiple_of(c * width, width), width)
            res = dot_tn(si[:, cols], sgu[...]).astype(BF)
            go_out[e, cols, :] = res[:, :FF]
            uo_out[e, cols, :] = res[:, FF:]
            return 0

        lax.fori_loop(0, D // width, chunk, 0)
        if e + 1 < NE:
            for c in saved(e + 1):
                c.start()

    def member(n, i, owner):
        m = meta[i].astype(F32)
        names, probs = m[:8], m[8:]
        row = lax.broadcasted_iota(jnp.int32, (8, T), 0)
        is_in = jnp.zeros((8, T), F32)
        prob = jnp.zeros((8, T), F32)
        for e in range(NE):
            here = names == (owner * NE + e).astype(F32)
            me = jnp.max(jnp.where(here, 1.0, 0.0), axis=0, keepdims=True)
            pe = jnp.sum(jnp.where(here, probs, 0.0), axis=0, keepdims=True)
            is_in = jnp.where(row == e, me, is_in)
            prob = jnp.where(row == e + 4, pe, prob)
        memb[n] = is_in
        slots[n] = prob

    def member_self(n, _):
        member(n, n, ep)
        return 0

    def member_near(l):
        parent = RAW[LEAF_PARENT[l]]

        def member_of(v, _):
            dy, dz = image_at(v, step(parent, LEAF[l]))
            owner = lax.rem(y + dy, 4) * 4 + lax.rem(z + dz, 4)
            member(16 + v * NL + l, source_at(v, parent), owner)
            return 0

        lax.fori_loop(0, 4, member_of, 0)

    def one_hot(n, _):
        spot = lax.broadcasted_iota(jnp.int32, (cap, T), 0).astype(F32)
        rows = [jnp.where(spot == slots[n, e : e + 1, :], 1.0, 0.0) for e in range(NE)]
        oh[n] = jnp.concatenate(rows, axis=0).astype(BF)
        return 0

    def prepare():
        lax.fori_loop(0, 16, member_self, 0)
        for l in range(NL):
            member_near(l)
        inside = memb[...].reshape(PAIRS * 8, T)
        rank = dot(inside.astype(BF), upper[...])
        row = lax.rem(lax.broadcasted_iota(jnp.int32, (PAIRS * 8, T), 0), 8)
        prob = slots[...].reshape(PAIRS * 8, T)
        slots[...] = jnp.where(row < 4, jnp.where(inside > 0.5, rank, -1.0), prob).reshape(PAIRS, 8, T)
        lax.fori_loop(0, PAIRS, one_hot, 0)

    def dispatch(b, node):
        slot = sum(BATCHES[b].index(source(v, node)) * 8**v for v in IMAGES)

        def bring(v, t):
            j = lax.rem(lax.div(jnp.int32(slot), t), 8)
            p, ch = lax.div(v, 2), lax.rem(v, 2)
            if node in RAW:
                piece = dot(oh[source_at(v, node)], raw[v, RAW.index(node)]).astype(BF)
            else:
                piece = cmp[v, LEAF.index(node)]
            rows = pl.ds(pl.multiple_of(j * pad, pad), pad)
            cols = pl.ds(pl.multiple_of(ch * HD, HD), HD)
            for k in range(NE // 2):
                xg[p, 2 * k, rows, cols] = piece[2 * cap * k : 2 * cap * k + pad]
                xg[p, 2 * k + 1, rows, cols] = piece[2 * cap * (k + 1) - pad : 2 * cap * (k + 1)]
            return t * 8

        lax.fori_loop(0, 4, bring, jnp.int32(1))

    def batch(b):
        code = sum(i * 16**j for j, i in enumerate(BATCHES[b]))
        count = len(BATCHES[b])
        used = pl.ds(0, count * pad)
        for i in BATCHES[b]:
            dispatch(b, (i // 4, i % 4))

        def weigh(j, t):
            i = lax.rem(lax.div(jnp.int32(code), t), 16)
            spot = lax.broadcasted_iota(jnp.int32, (cap, T), 0).astype(F32)
            for e in range(NE):
                hit = spot == slots[i, e : e + 1, :]
                weight = jnp.sum(
                    jnp.where(hit, slots[i, e + 4 : e + 5, :], 0.0), axis=1, keepdims=True
                )
                rows = pl.ds(pl.multiple_of(j * pad + e % 2 * (pad - cap), 8), cap)
                pv[e, rows, :] = jnp.broadcast_to(weight, (cap, 128))
            return t * 16

        lax.fori_loop(0, count, weigh, jnp.int32(1))

        def expert(e, _):
            gate_up = dot(xg[1, e, used, :], wgu[e])
            gate, up = gate_up[:, :FF], gate_up[:, FF:]
            hg = dot_nt(xg[0, e, used, :], wd[e])
            sigma = jax.nn.sigmoid(gate)
            active = gate * sigma
            hidden = (active * up).astype(BF).astype(F32)
            slot_prob = jnp.sum(hidden * hg, axis=1, keepdims=True)
            sp[e, used, :] = jnp.broadcast_to(slot_prob, (count * pad, 128))
            scaled = hg * pv[e, used, :][:, :1]
            gg = (scaled * up * sigma * (1.0 + gate * (1.0 - sigma))).astype(BF)
            ug = (scaled * active).astype(BF)
            xg[1, e, used, :] = dot_nt(jnp.concatenate([gg, ug], axis=1), wgu[e]).astype(BF)
            return 0

        lax.fori_loop(0, NE, expert, 0)

        def finish(j, t):
            i = lax.rem(lax.div(jnp.int32(code), t), 16)
            rows = pl.ds(pl.multiple_of(j * pad, pad), pad)
            cut = cap // 16 * 16
            for k in range(NE // 2):
                even, odd = xg[1, 2 * k, rows, :], xg[1, 2 * k + 1, rows, :]
                middle = jnp.concatenate(
                    [even[cut:].astype(F32)[:8], odd[:16].astype(F32)[8:]], axis=0
                ).astype(BF)
                o = 2 * cap * k
                srows[i, o : o + cut, :] = even[:cut]
                srows[i, o + cut : o + cut + 16, :] = middle
                srows[i, o + cut + 16 : o + 2 * cap, :] = odd[16:]
            spot = lax.broadcasted_iota(jnp.int32, (cap, T), 0).astype(F32)
            names = meta[i].astype(F32)[:8]
            out = jnp.zeros((8, T), F32)
            for e in range(NE):
                hit = spot == slots[i, e : e + 1, :]
                part = pl.ds(pl.multiple_of(j * pad + e % 2 * (pad - cap), 8), cap)
                val = jnp.sum(jnp.where(hit, sp[e, part, :][:, :1], 0.0), axis=0, keepdims=True)
                out = jnp.where(names == (ep * NE + e).astype(F32), val, out)
            ppg[i] = out.astype(BF)
            return t * 16

        lax.fori_loop(0, count, finish, jnp.int32(1))

    def leaf_up(v, l):
        return copy(
            ("up_leaf", v, l), srows.at[source(v, LEAF[l]), :, pl.ds(v * QD, QD)], fr.at[v, l],
            toward(v, LEAF[l], RAW[LEAF_PARENT[l]]),
        )

    def raw_up(v, k, c):
        rows = pl.ds(c * TC, TC)
        return copy(
            ("up_raw", v, k, c), pm.at[v, k - 1, rows], nm.at[v, k - 1, rows],
            toward(v, RAW[k], RAW[RAW_PARENT[k]]),
        )

    def return_leaf(*ls):
        for l in ls:
            for v in IMAGES:
                start(leaf_up(v, l))

    def children(k):
        return [l for l in range(NL) if LEAF_PARENT[l] == k], [c for c in range(1, len(RAW)) if RAW_PARENT[c] == k]

    def gathered(k, c, v, i, cols):
        leaves, raws = children(k)
        rows = pl.ds(c * TC, TC)
        lhs = jnp.concatenate([oh[i, :, rows]] + [oh[16 + v * NL + l, :, rows] for l in leaves], axis=0)
        rhs = jnp.concatenate([srows[i, :, cols]] + [fr[v, l] for l in leaves], axis=0)
        res = dot_tn(lhs, rhs)
        for r in raws:
            res = res + nm[v, r - 1, rows, :].astype(F32)
        return res

    def wait_children(k, c, v):
        leaves, raws = children(k)
        if c == 0:
            for l in leaves:
                leaf_up(v, l).wait_recv()
        for r in raws:
            raw_up(v, r, c).wait_recv()

    def merge(k, c):
        for v in IMAGES:
            wait_children(k, c, v)

        def add(v, _):
            cols = pl.ds(pl.multiple_of(v * QD, QD), QD)
            pm[v, k - 1, pl.ds(c * TC, TC), :] = gathered(k, c, v, source_at(v, RAW[k]), cols).astype(BF)
            return 0

        lax.fori_loop(0, 4, add, 0)
        for v in IMAGES:
            start(raw_up(v, k, c))

    weight_grads(0)
    for c in ms:
        c.wait_recv()
    prepare()
    send_leaf(0, 1)
    pass_raw(1, 3)
    pass_raw(2, 4)
    send_leaf(3)
    weight_grads(1)
    for c in weights:
        c.wait()
    wait_leaf(0, 1)
    batch(0)
    wait_raw(3)
    pass_raw(4, 5)
    send_leaf(4, 2)
    weight_grads(2)
    wait_raw(5)
    send_leaf(8, 9)
    send_leaf(5, 6, 7)
    wait_leaf(3, 4)
    batch(1)
    return_leaf(3, 4)
    weight_grads(3)
    wait_leaf(2, 8, 9)
    batch(2)
    return_leaf(8, 9, 2)
    wait_leaf(5, 6, 7)
    batch(3)
    return_leaf(5, 6)
    merge(5, 0)
    merge(5, 1)
    return_leaf(7)
    merge(3, 0)
    merge(3, 1)
    return_leaf(0, 1)
    merge(4, 0)
    merge(1, 0)
    merge(4, 1)
    merge(2, 0)
    merge(1, 1)
    pgs = [copy(("c", i), ppg.at[i], ppgr.at[mirror[i]], peers[i]) for i in range(1, 16)]
    for c in pgs:
        start(c)
    merge(2, 1)
    ups = {}
    for c in range(CHUNKS):
        for v in IMAGES:
            rows, cols = pl.ds(c * TC, TC), pl.ds(v * QD, QD)
            wait_children(0, c, v)
            upv[rows, cols] = gathered(0, c, v, 0, cols).astype(BF)
            ups[v, c] = copy(("up", v, c), upv.at[rows, cols], up_out.at[rows, cols], before)

            @pl.when(sec > 0)
            def _():
                ups[v, c].start()

    for c in pgs:
        c.wait_recv()
    routed = ppg[0].astype(F32)
    for i in range(1, 16):
        routed = routed + ppgr[i].astype(F32)
    pg_out[...] = routed

    for c in sent:
        c.wait_send()
    for c in ups.values():
        @pl.when(sec > 0)
        def _():
            c.wait_send()

        @pl.when(sec < sections - 1)
        def _():
            c.wait_recv()


def deliver(up_in, pg_in, go_in, uo_in, up_out, pg_out, go_out, uo_out, sem):
    out = [(up_in, up_out)]
    for e in range(go_in.shape[0]):
        out += [(go_in.at[e], go_out.at[e]), (uo_in.at[e], uo_out.at[e])]
    out = [pltpu.make_async_copy(v, o, sem.at[k]) for k, (v, o) in enumerate(out)]
    for c in out:
        c.start()
    pg_out[...] = pg_in[...].astype(BF)
    for c in out:
        c.wait()


def per_device(sections, og, li, ids, probs, wg, wu, wd, si, sg, su, counts):
    T, D = og.shape[1], og.shape[2]
    NE, FF = wg.shape[1], wg.shape[3]
    SL = si.shape[2]
    cap = SL // 16
    pad = -(-cap // 16) * 16
    M, R = NE * cap, max(map(len, BATCHES)) * pad
    HD, QD = D // 2, D // 4
    hbm = pl.BlockSpec(memory_space=pl.ANY)
    V = pltpu.VMEM
    up, pg, go, uo = pl.pallas_call(
        functools.partial(kernel, sections, cap, pad),
        out_shape=(
            V((T, D), BF),
            V((8, T), F32),
            V((NE, D, FF), BF),
            V((NE, D, FF), BF),
        ),
        in_specs=[hbm] * 2 + [pl.BlockSpec(memory_space=V)] * 2 + [hbm] * 6 + [pl.BlockSpec(memory_space=pltpu.SMEM)],
        out_specs=(pl.BlockSpec(memory_space=V),) * 4,
        scratch_shapes=[
            V((4, len(RAW), T, HD), BF), V((4, NL, M, HD), BF), V((4, NL, M, HD), BF),
            V((16, 16, T), BF), V((NE, D, 2 * FF), BF), V((NE, FF, D), BF),
            V((SL, D), BF), V((2, SL, FF), BF), V((SL, 2 * FF), BF),
            V((PAIRS, 8, T), F32), V((PAIRS, 8, T), F32), V((T, T), BF), V((PAIRS, M, T), BF),
            V((2, NE, R, D), BF), V((NE, R, 128), F32), V((NE, R, 128), F32), V((16, M, D), BF),
            V((4, NL, M, QD), BF), V((4, len(RAW) - 1, T, QD), BF), V((4, len(RAW) - 1, T, QD), BF),
            V((T, D), BF), V((16, 8, T), BF), V((16, 8, T), BF),
            pltpu.SemaphoreType.DMA((N_SEMS,)), pltpu.SemaphoreType.DMA((N_SEMS,)),
            pltpu.SemaphoreType.DMA((14,)),
        ],
        compiler_params=pltpu.CompilerParams(
            collective_id=0, has_side_effects=True, vmem_limit_bytes=59_800_000
        ),
    )(og[0], li[0], ids[0].T, probs[0].T, wg[0], wu[0], wd[0], si[0], sg[0], su[0], counts[0])
    up, pg, go, uo = pl.pallas_call(
        deliver,
        out_shape=(
            jax.ShapeDtypeStruct((T, D), BF),
            jax.ShapeDtypeStruct((8, T), BF),
            jax.ShapeDtypeStruct((NE, D, FF), BF),
            jax.ShapeDtypeStruct((NE, D, FF), BF),
        ),
        in_specs=[pl.BlockSpec(memory_space=V)] * 4,
        out_specs=(hbm, pl.BlockSpec(memory_space=V), hbm, hbm),
        scratch_shapes=[pltpu.SemaphoreType.DMA((1 + 2 * NE,))],
        compiler_params=pltpu.CompilerParams(vmem_limit_bytes=16 * 2**20),
    )(up, pg, go, uo)
    return up[None], pg.T[None], go[None], uo[None]


def solution(mesh):
    return jax.shard_map(
        functools.partial(per_device, mesh.shape["section"]),
        mesh=mesh,
        in_specs=(
            P("section", "ep", None),
            P("section", "ep", None),
            P("section", "ep", None),
            P("section", "ep", None),
            P("section", "ep", None, None),
            P("section", "ep", None, None),
            P("section", "ep", None, None),
            P("section", "ep", None, None),
            P("section", "ep", None, None),
            P("section", "ep", None, None),
            P("section", "ep", None),
        ),
        out_specs=(
            P("section", "ep", None),
            P("section", "ep", None),
            P("section", "ep", None, None),
            P("section", "ep", None, None),
        ),
        check_vma=False,
    )
```

time: 130 us -> 123 us (0.946)
  Pallas kernels: 129 us -> 122 us
    pallas_call x1, Pallas kernels: 125 us -> 119 us  [per_device(): pl.pallas_call(functools.partial(kernel, sections, cap, pad), out_shape=(...]
where the time goes in v3:
time: 123 us
  Pallas kernels  122 us (99%)
    pallas_call x1, Pallas kernels, per_device(): pl.pallas_call(functools.partial(kernel, sections, cap, pad), out_shape=(...  119 us
    pallas_call x1, Pallas kernels, per_device(): pl.pallas_call(deliver, out_shape=(jax.ShapeDtypeStruct((T, D), BF), jax....  3.49 us

profile of v3, /device:TPU:1, one launch (start us, length us, event | category | flops | bytes accessed | tf_op | source)
XLA Modules:
  0.0 122.9 jit_solution(13157385719929867927)
XLA Ops:
  0.6 118.7 %shard_map.138 = (bf16[256,1024]{1,0:T(8,128)(2,1)S(1)}, f32[8,256]{1,0:T(8,128)S(1)}, bf16[4,1024,384]{2,1,0:T(8,128)(2,1)S(1)}, bf16[4,1024,384]{2,1,0:T(8,128)(2,1)S(1)}) custom-call(bf16[256,1024]{1,0:T(8,128)(2,1)} %bitcast.27, bf16[256,1024]{1,0:T(8,128)(2,1)} %bitcast.28, s32[8,256]{1,0:T(8,128)} %bitcast.29, bf16[8,256]{1,0:T(8,128)(2,1)} %bitcast.30, ...), custom_call_target="tpu_custom_call" | custom-call | tf_op jit(solution)/shard_map/pallas_call | solution.py:499
  119.4 3.5 %shard_map.139 = (bf16[256,1024]{1,0:T(8,128)(2,1)}, bf16[8,256]{1,0:T(8,128)(2,1)}, bf16[4,1024,384]{2,1,0:T(8,128)(2,1)}, bf16[4,1024,384]{2,1,0:T(8,128)(2,1)}) custom-call(bf16[256,1024]{1,0:T(8,128)(2,1)S(1)} %get-tuple-element.12.up_in, f32[8,256]{1,0:T(8,128)S(1)} %get-tuple-element.13.pg_in, bf16[4,1024,384]{2,1,0:T(8,128)(2,1)S(1)} %get-tuple-element.14.go_in, ...), custom_call_target="tpu_custom_call" | custom-call | tf_op jit(solution)/shard_map/pallas_call | solution.py:524

commit v4 on v3

--- a/solution.py
+++ b/solution.py
@@ -37,6 +37,10 @@
 
 def minus(node):
     return (-node[0]) % 4, (-node[1]) % 4
+
+
+def parent_of(node):
+    return RAW[RAW_PARENT[RAW.index(node)] if node in RAW else LEAF_PARENT[LEAF.index(node)]]
 
 
 def step(parent, child):
@@ -79,8 +83,6 @@
     def at(yy, zz):
         return {"ep": lax.rem(yy, 4) * 4 + lax.rem(zz, 4)}
 
-    peers = {i: at(y + i // 4, z + i % 4) for i in range(1, 16)}
-    mirror = {i: (4 - i // 4) % 4 * 4 + (4 - i % 4) % 4 for i in range(1, 16)}
     before = {"section": lax.rem(sec + sections - 1, sections)}
     after = {"section": lax.rem(sec + 1, sections)}
 
@@ -121,14 +123,16 @@
         ]
 
     barrier = pltpu.get_barrier_semaphore()
-    for dev in (*peers.values(), before, after):
+    for dev in (at(y + 1, z), at(y + 3, z), at(y, z + 1), at(y, z + 3), before, after):
         pl.semaphore_signal(barrier, inc=1, device_id=dev, device_id_type=MESH)
     for c in saved(0):
         c.start()
     for c in weights:
         c.start()
     meta[0] = jnp.concatenate([ids_in[...].astype(F32), prob_in[...].astype(F32)], axis=0).astype(BF)
-    pl.semaphore_wait(barrier, 17)
+    memb[...] = jnp.zeros(memb.shape, F32)
+    slots[...] = jnp.zeros(slots.shape, F32)
+    pl.semaphore_wait(barrier, 6)
     for c in own:
         c.wait()
 
@@ -154,7 +158,7 @@
     def send_leaf(*ls):
         for l in ls:
             def pick(v, _):
-                sendc[v, l] = dot(oh[16 + v * NL + l], raw[v, LEAF_PARENT[l]]).astype(BF)
+                sendc[v, l] = dot(oh[16 + 4 * l + v], raw[v, LEAF_PARENT[l]]).astype(BF)
                 return 0
 
             lax.fori_loop(0, 4, pick, 0)
@@ -176,21 +180,35 @@
             raw_down(v, k).wait_recv()
             start(raw_down(v, child))
 
-    ms = [copy(("m", i), meta.at[0], meta.at[mirror[i]], peers[i]) for i in range(1, 16)]
-    for c in ms:
-        start(c)
-    for k in (1, 2):
+    def meta_down(node):
+        parent = parent_of(node)
+        return copy(
+            ("meta", node), meta.at[source(0, parent)], meta.at[source(0, node)], toward(0, parent, node)
+        )
+
+    def send_meta(*nodes):
+        for node in nodes:
+            start(meta_down(node))
+
+    def wait_meta(*nodes):
+        for node in nodes:
+            meta_down(node).wait_recv()
+
+    def send_raw(k):
         for v in IMAGES:
             start(raw_down(v, k))
 
-    @pl.when(sec == sections - 1)
-    def _():
-        up_out[...] = jnp.zeros(up_out.shape, BF)
-
-    upper[...] = jnp.where(
-        lax.broadcasted_iota(jnp.int32, (T, T), 0) < lax.broadcasted_iota(jnp.int32, (T, T), 1), 1.0, 0.0
-    ).astype(BF)
-    pv[...] = jnp.zeros(pv.shape, F32)
+    send_meta((0, 1), (1, 0), (0, 3), (3, 0))
+
+    def clear():
+        @pl.when(sec == sections - 1)
+        def _():
+            up_out[...] = jnp.zeros(up_out.shape, BF)
+
+        upper[...] = jnp.where(
+            lax.broadcasted_iota(jnp.int32, (T, T), 0) < lax.broadcasted_iota(jnp.int32, (T, T), 1), 1.0, 0.0
+        ).astype(BF)
+        pv[...] = jnp.zeros(pv.shape, F32)
 
     def weight_grads(e):
         for c in saved(e):
@@ -231,17 +249,13 @@
         memb[n] = is_in
         slots[n] = prob
 
-    def member_self(n, _):
-        member(n, n, ep)
-        return 0
-
     def member_near(l):
         parent = RAW[LEAF_PARENT[l]]
 
         def member_of(v, _):
             dy, dz = image_at(v, step(parent, LEAF[l]))
             owner = lax.rem(y + dy, 4) * 4 + lax.rem(z + dz, 4)
-            member(16 + v * NL + l, source_at(v, parent), owner)
+            member(16 + 4 * l + v, source_at(v, parent), owner)
             return 0
 
         lax.fori_loop(0, 4, member_of, 0)
@@ -252,16 +266,20 @@
         oh[n] = jnp.concatenate(rows, axis=0).astype(BF)
         return 0
 
-    def prepare():
-        lax.fori_loop(0, 16, member_self, 0)
-        for l in range(NL):
+    def prepare(sources, leaves):
+        for i in sources:
+            member(i, i, ep)
+        for l in leaves:
             member_near(l)
         inside = memb[...].reshape(PAIRS * 8, T)
         rank = dot(inside.astype(BF), upper[...])
         row = lax.rem(lax.broadcasted_iota(jnp.int32, (PAIRS * 8, T), 0), 8)
         prob = slots[...].reshape(PAIRS * 8, T)
         slots[...] = jnp.where(row < 4, jnp.where(inside > 0.5, rank, -1.0), prob).reshape(PAIRS, 8, T)
-        lax.fori_loop(0, PAIRS, one_hot, 0)
+        for i in sources:
+            one_hot(i, 0)
+        if leaves:
+            lax.fori_loop(16 + 4 * leaves[0], 20 + 4 * leaves[-1], one_hot, 0)
 
     def dispatch(b, node):
         slot = sum(BATCHES[b].index(source(v, node)) * 8**v for v in IMAGES)
@@ -370,7 +388,7 @@
     def gathered(k, c, v, i, cols):
         leaves, raws = children(k)
         rows = pl.ds(c * TC, TC)
-        lhs = jnp.concatenate([oh[i, :, rows]] + [oh[16 + v * NL + l, :, rows] for l in leaves], axis=0)
+        lhs = jnp.concatenate([oh[i, :, rows]] + [oh[16 + 4 * l + v, :, rows] for l in leaves], axis=0)
         rhs = jnp.concatenate([srows[i, :, cols]] + [fr[v, l] for l in leaves], axis=0)
         res = dot_tn(lhs, rhs)
         for r in raws:
@@ -398,15 +416,44 @@
         for v in IMAGES:
             start(raw_up(v, k, c))
 
+    nodes = RAW[1:] + LEAF
+
+    def pg_up(node):
+        parent = parent_of(node)
+        return copy(
+            ("pg", node), ppg.at[source(0, node)], ppgr.at[nodes.index(node)], toward(0, node, parent)
+        )
+
+    def merge_pg(k):
+        i = source(0, RAW[k])
+        res = ppg[i].astype(F32)
+        for node in nodes:
+            if parent_of(node) == RAW[k]:
+                pg_up(node).wait_recv()
+                res = res + ppgr[nodes.index(node)].astype(F32)
+        if k == 0:
+            pg_out[...] = res
+        else:
+            ppg[i] = res.astype(BF)
+            start(pg_up(RAW[k]))
+
+    send_raw(1)
+    wait_meta((0, 1), (1, 0))
+    send_meta((0, 2), (1, 1), (3, 1), (2, 0), (1, 3))
+    send_raw(2)
+    clear()
+    wait_meta((0, 3), (3, 0))
+    prepare((0, 1, 3, 4, 12), range(0, 5))
+    send_leaf(0, 1)
     weight_grads(0)
-    for c in ms:
-        c.wait_recv()
-    prepare()
-    send_leaf(0, 1)
+    wait_meta((0, 2), (2, 0))
+    send_meta((1, 2), (3, 2), (2, 3), (2, 1))
     pass_raw(1, 3)
     pass_raw(2, 4)
     send_leaf(3)
     weight_grads(1)
+    wait_meta((2, 3))
+    send_meta((2, 2), (3, 3))
     for c in weights:
         c.wait()
     wait_leaf(0, 1)
@@ -414,34 +461,42 @@
     wait_raw(3)
     pass_raw(4, 5)
     send_leaf(4, 2)
-    weight_grads(2)
+    wait_meta((1, 1), (3, 1), (1, 3), (1, 2), (3, 2), (2, 1))
+    prepare((2, 8, 7, 13, 15, 6, 14, 9, 11), range(5, 10))
     wait_raw(5)
     send_leaf(8, 9)
     send_leaf(5, 6, 7)
     wait_leaf(3, 4)
     batch(1)
     return_leaf(3, 4)
-    weight_grads(3)
+    weight_grads(2)
+    wait_meta((2, 2), (3, 3))
+    prepare((5, 10), ())
     wait_leaf(2, 8, 9)
     batch(2)
     return_leaf(8, 9, 2)
+    weight_grads(3)
     wait_leaf(5, 6, 7)
     batch(3)
     return_leaf(5, 6)
+    for node in LEAF:
+        start(pg_up(node))
     merge(5, 0)
     merge(5, 1)
     return_leaf(7)
+    merge_pg(5)
     merge(3, 0)
     merge(3, 1)
+    merge_pg(3)
     return_leaf(0, 1)
     merge(4, 0)
     merge(1, 0)
     merge(4, 1)
+    merge_pg(4)
+    merge_pg(1)
     merge(2, 0)
     merge(1, 1)
-    pgs = [copy(("c", i), ppg.at[i], ppgr.at[mirror[i]], peers[i]) for i in range(1, 16)]
-    for c in pgs:
-        start(c)
+    merge_pg(2)
     merge(2, 1)
     ups = {}
     for c in range(CHUNKS):
@@ -455,12 +510,7 @@
             def _():
                 ups[v, c].start()
 
-    for c in pgs:
-        c.wait_recv()
-    routed = ppg[0].astype(F32)
-    for i in range(1, 16):
-        routed = routed + ppgr[i].astype(F32)
-    pg_out[...] = routed
+    merge_pg(0)
 
     for c in sent:
         c.wait_send()
@@ -518,7 +568,7 @@
             pltpu.SemaphoreType.DMA((14,)),
         ],
         compiler_params=pltpu.CompilerParams(
-            collective_id=0, has_side_effects=True, vmem_limit_bytes=59_800_000
+            collective_id=0, has_side_effects=True, vmem_limit_bytes=60_150_000
         ),
     )(og[0], li[0], ids[0].T, probs[0].T, wg[0], wu[0], wd[0], si[0], sg[0], su[0], counts[0])
     up, pg, go, uo = pl.pallas_call(

time: 123 us -> 122 us (level)
    pallas_call x1, Pallas kernels: 119 us -> 117 us  [per_device(): pl.pallas_call(functools.partial(kernel, sections, cap, pad), out_shape=(...]
where the time goes in v4:
time: 122 us
  Pallas kernels  121 us (99%)
    pallas_call x1, Pallas kernels, per_device(): pl.pallas_call(functools.partial(kernel, sections, cap, pad), out_shape=(...  117 us
    pallas_call x1, Pallas kernels, per_device(): pl.pallas_call(deliver, out_shape=(jax.ShapeDtypeStruct((T, D), BF), jax....  3.49 us

profile of v4, /device:TPU:1, one launch (start us, length us, event | category | flops | bytes accessed | tf_op | source)
XLA Modules:
  0.0 121.7 jit_solution(14983131762748824341)
XLA Ops:
  0.6 117.4 %shard_map.138 = (bf16[256,1024]{1,0:T(8,128)(2,1)S(1)}, f32[8,256]{1,0:T(8,128)S(1)}, bf16[4,1024,384]{2,1,0:T(8,128)(2,1)S(1)}, bf16[4,1024,384]{2,1,0:T(8,128)(2,1)S(1)}) custom-call(bf16[256,1024]{1,0:T(8,128)(2,1)} %bitcast.27, bf16[256,1024]{1,0:T(8,128)(2,1)} %bitcast.28, s32[8,256]{1,0:T(8,128)} %bitcast.29, bf16[8,256]{1,0:T(8,128)(2,1)} %bitcast.30, ...), custom_call_target="tpu_custom_call" | custom-call | tf_op jit(solution)/shard_map/pallas_call | solution.py:549
  118.0 3.5 %shard_map.139 = (bf16[256,1024]{1,0:T(8,128)(2,1)}, bf16[8,256]{1,0:T(8,128)(2,1)}, bf16[4,1024,384]{2,1,0:T(8,128)(2,1)}, bf16[4,1024,384]{2,1,0:T(8,128)(2,1)}) custom-call(bf16[256,1024]{1,0:T(8,128)(2,1)S(1)} %get-tuple-element.12.up_in, f32[8,256]{1,0:T(8,128)S(1)} %get-tuple-element.13.pg_in, bf16[4,1024,384]{2,1,0:T(8,128)(2,1)S(1)} %get-tuple-element.14.go_in, ...), custom_call_target="tpu_custom_call" | custom-call | tf_op jit(solution)/shard_map/pallas_call | solution.py:574
